TPU v7x, 768 devices: a whole 4x8x12 slice. The times are simulated.
768 devices in a mesh: grp: 16 (over y, core), sub: 48 (over z, x).
Axes of the slice: x: 4, y: 8, z: 12, core: 2. Of those that a mesh axis runs over, the one named last changes fastest.
Arguments:
- fields: float32 [4, 35, 196608], P(None, None, ('grp', 'sub')), may hold values from -6 to 6
- section_store: float32 [4, 35, 196608], P(None, None, ('grp', 'sub')), may hold values from -6 to 6
- metric_terms: float32 [9, 196608], P(None, ('grp', 'sub')), may hold values from -6 to 6
- normals: float32 [4, 3, 196608], P(None, None, ('grp', 'sub')), may hold values from -3 to 3
- face_scale: float32 [4, 196608], P(None, ('grp', 'sub')), may hold values from 1 to 4
- damping: float32 [196608], P(('grp', 'sub')), may hold values from 1 to 10
- absorb_mask: int32 [196608], P(('grp', 'sub')), may hold values from 0 to 1
- refine_level: int32 [196608], P(('grp', 'sub')), may hold values from 0 to 2
- face_source: int32 [4, 196608], P(None, ('grp', 'sub')), may hold values from -1 to 2623, as said below
- orientation: int32 [4, 196608], P(None, ('grp', 'sub')), may hold values from 0 to 5, as said below
- derivative: float32 [3, 35, 35], replicated, may hold values from -1 to 1
- lift_matrix: float32 [35, 60], replicated, may hold values from -0.75 to 0.75
Outputs:
- fields_next: float32 [4, 35, 196608], P(None, None, ('grp', 'sub'))
- store_next: float32 [4, 35, 196608], P(None, None, ('grp', 'sub'))
- absorbed_energy: float32 [], replicated
Inputs may be any that keep to these rules, and one draw needn't show every extreme that they name: `face_source`: A device uses the slots of a block from rank 0 on without gaps; it never uses block s (its own sub index), nor block 48 at the first grp index or block 49 at the last. For a sub peer b with |b - s| <= 4 at most 32 ranks are used, for other peers at most 8, and across grp at most 32; in every draw some near pair uses all 32, some farther pair all 8, and some pair across grp all 32. Local neighbours lie on the same device. `orientation`: paired faces have inverse orientations: 1 and 2 swap, 0, 3, 4 and 5 stay.
All inputs are finite; a program needn't handle non-finite values.
Results may differ from a plain program's by a relative error of at most 0.0003.
Values sent between devices are 32-bit elements; how exact they have to be, the bound alone decides.
A program may use at most 32 MiB of HBM per device.

v0:
```python
import jax
import jax.numpy as jnp
import numpy as np
from jax import lax
from jax.sharding import Mesh
from jax.sharding import PartitionSpec as P

VOLUME_NODES = 35
FACE_NODES = 15
SUB = ("sub_0", "sub_1")
GRP = ("grp_0", "grp_1")
GRP_SUB = ("grp_0", "grp_1", "sub_0", "sub_1")


RUNGE_CARRY = -567301805773.0 / 1357537059087.0
RUNGE_ADVANCE = 5161836677717.0 / 13612068292357.0
TIME_STEP = 0.02


def passed_along(value, axis, steps):
    count = lax.axis_size(axis)
    first, last = (max(0, -steps), min(count, count - steps))
    return lax.ppermute(value, axis, [(source, source + steps) for source in range(first, last)])


def by_axis(value, axes):
    for axis in axes:
        value = lax.psum(value, axis)
    return value


def node_tables():
    volume_list = [
        (first_part, second_part, third_part, 4 - first_part - second_part - third_part)
        for first_part in range(5)
        for second_part in range(5 - first_part)
        for third_part in range(5 - first_part - second_part)
    ]
    triples = [
        (first_part, second_part, 4 - first_part - second_part)
        for first_part in range(5)
        for second_part in range(5 - first_part)
    ]
    face_index = np.zeros((4, 15), np.int32)
    for facet in range(4):
        others = [corner for corner in range(4) if corner != facet]
        for node_pos in range(15):
            corners = [0, 0, 0, 0]
            for place_pos in range(3):
                corners[others[place_pos]] = triples[node_pos][place_pos]
            face_index[facet, node_pos] = volume_list.index(tuple(corners))
    vertex_orders = [(0, 1, 2), (1, 2, 0), (2, 0, 1), (0, 2, 1), (2, 1, 0), (1, 0, 2)]
    turn_index = np.zeros((6, 15), np.int32)
    for option in range(6):
        vertex_order = vertex_orders[option]
        for node_pos in range(15):
            triple = triples[node_pos]
            turned = (triple[vertex_order[0]], triple[vertex_order[1]], triple[vertex_order[2]])
            turn_index[option, node_pos] = triples.index(turned)
    return (face_index, turn_index)


def turn_matrices():
    face_index, turn_index = node_tables()
    table = np.zeros((6, 15, 15), np.float32)
    for option in range(6):
        for node_pos in range(15):
            table[option, node_pos, turn_index[option, node_pos]] = 1.0
    return jnp.asarray(table, jnp.float32)


def pick_matrix():
    face_index, turn_index = node_tables()
    table = np.zeros((60, 35), np.float32)
    for node_pos in range(15):
        for facet in range(4):
            table[node_pos * 4 + facet, face_index[facet, node_pos]] = 1.0
    return jnp.asarray(table, jnp.float32)


def advance(
    fields,
    section_store,
    metric_terms,
    normals,
    face_scale,
    damping,
    absorb_mask,
    refine_level,
    face_codes,
    orient_flat,
    inner_cols,
    outer_cols,
    derivative,
    lift_matrix,
):
    elements_here = fields.shape[2]
    total_faces = 4 * elements_here
    turning = turn_matrices()
    inside = inner_cols.reshape(4, FACE_NODES, total_faces)
    gathered = outer_cols.reshape(4, FACE_NODES, total_faces)
    outside = gathered
    for option in range(1, 6):
        turned = jnp.einsum(
            "jk,ckx->cjx", turning[option], gathered, precision=lax.Precision.HIGHEST
        )
        outside = jnp.where(orient_flat[None, None, :] == option, turned, outside)
    normal_flat = jnp.transpose(normals, (1, 0, 2)).reshape(3, total_faces)
    on_wall = (face_codes < 0)[None, :]
    press_in = inside[0]
    veloc_in = inside[1:]
    normal_in = jnp.sum(normal_flat[:, None, :] * veloc_in, 0)
    press_out = jnp.where(on_wall, press_in, outside[0])
    veloc_out = jnp.where(
        on_wall[None], veloc_in - 2.0 * normal_flat[:, None, :] * normal_in[None], outside[1:]
    )
    press_jump = press_in - press_out
    normal_jump = jnp.sum(normal_flat[:, None, :] * (veloc_in - veloc_out), 0)
    growth = jnp.exp2(refine_level.astype(jnp.float32))
    weight_face = (face_scale * growth[None, :]).reshape(total_faces)
    flux_press = 0.5 * weight_face[None, :] * (normal_jump - press_jump)
    flux_veloc = (
        0.5
        * weight_face[None, None, :]
        * normal_flat[:, None, :]
        * (press_jump - normal_jump)[None]
    )
    flux_all = jnp.concatenate([flux_press[None], flux_veloc], 0).reshape(
        4, FACE_NODES, 4, elements_here
    )
    lifted = jnp.einsum(
        "nfj,cjfe->cne",
        lift_matrix.reshape(VOLUME_NODES, 4, FACE_NODES),
        flux_all,
        precision=lax.Precision.HIGHEST,
    )
    slopes = jnp.einsum("dnm,cme->dcne", derivative, fields, precision=lax.Precision.HIGHEST)
    metric = metric_terms.reshape(3, 3, elements_here) * growth[None, None, :]
    physical = jnp.einsum("ide,dcne->icne", metric, slopes, precision=lax.Precision.HIGHEST)
    absorb = damping * absorb_mask.astype(jnp.float32)
    diverge = physical[0, 1] + physical[1, 2] + physical[2, 3]
    volume = jnp.concatenate([-diverge[None], -physical[:, 0]], 0)
    change = volume + lifted - absorb[None, None, :] * fields
    store_next = RUNGE_CARRY * section_store + TIME_STEP * change
    fields_next = fields + RUNGE_ADVANCE * store_next
    energy = jnp.sum(absorb * jnp.sum(fields_next * fields_next, (0, 1)))
    return (fields_next, store_next, energy)


def local(
    fields,
    section_store,
    metric_terms,
    normals,
    face_scale,
    damping,
    absorb_mask,
    refine_level,
    face_source,
    orientation,
    derivative,
    lift_matrix,
):
    elements_here = fields.shape[2]
    total_faces = 4 * elements_here
    slot_width = elements_here // 8
    peer_count = lax.axis_size(SUB)
    block_total = peer_count + 2
    row_count = 4 * FACE_NODES
    picker = pick_matrix()
    traces = jnp.einsum("kn,cne->cke", picker, fields, precision=lax.Precision.HIGHEST)
    inner_cols = traces.reshape(row_count, total_faces)
    face_codes = face_source.reshape(total_faces)
    orient_flat = orientation.reshape(total_faces)
    remote = face_codes >= total_faces
    slot_index = jnp.where(remote, face_codes - total_faces, 0)
    block_index = jnp.where(remote, slot_index // slot_width, block_total)
    within = slot_index % slot_width
    outbox = (
        jnp.zeros((block_total, row_count, slot_width), jnp.float32)
        .at[block_index, :, within]
        .set(inner_cols.T, mode="drop")
    )
    arrived = lax.all_to_all(outbox[:peer_count], SUB, split_axis=0, concat_axis=0, tiled=True)
    from_below = passed_along(outbox[peer_count + 1], GRP, 1)
    from_above = passed_along(outbox[peer_count], GRP, -1)
    received = jnp.concatenate([arrived, from_below[None], from_above[None]], 0)
    local_side = (face_codes >= 0) & (face_codes < total_faces)
    own_pick = jnp.take(inner_cols, jnp.clip(face_codes, 0, total_faces - 1), axis=1)
    far_pick = received[jnp.minimum(block_index, block_total - 1), :, within].T
    outer_cols = jnp.where(local_side[None, :], own_pick, jnp.where(remote[None, :], far_pick, 0.0))
    fields_next, store_next, energy = advance(
        fields,
        section_store,
        metric_terms,
        normals,
        face_scale,
        damping,
        absorb_mask,
        refine_level,
        face_codes,
        orient_flat,
        inner_cols,
        outer_cols,
        derivative,
        lift_matrix,
    )
    summed = by_axis(energy, GRP_SUB)
    divisor = elements_here * lax.axis_size(GRP) * peer_count * VOLUME_NODES
    return (fields_next, store_next, summed / divisor)


def solution(mesh):
    torus = Mesh(mesh.devices.reshape(8, 2, 12, 4), ("grp_0", "grp_1", "sub_0", "sub_1"))
    in_specs = (
        P(None, None, GRP_SUB),
        P(None, None, GRP_SUB),
        P(None, GRP_SUB),
        P(None, None, GRP_SUB),
        P(None, GRP_SUB),
        P(GRP_SUB),
        P(GRP_SUB),
        P(GRP_SUB),
        P(None, GRP_SUB),
        P(None, GRP_SUB),
        P(),
        P(),
    )
    out_specs = (P(None, None, GRP_SUB), P(None, None, GRP_SUB), P())
    return jax.shard_map(local, mesh=torus, in_specs=in_specs, out_specs=out_specs, check_vma=False)
```

profile of v0, /device:TPU:40, one launch (start us, length us, event | category | flops | bytes accessed | tf_op | source)
XLA Modules:
  0.0 129.9 jit_solution(8412613775752986612)
XLA Ops:
  0.6 1.3 broadcast_compare_fusion.6
  1.9 0.7 clamp_bitcast_fusion.1
  2.7 0.7 multiply_reduce_fusion.2
  3.5 0.8 and_reduce_fusion
  4.2 1.3 %convolution_bitcast_fusion.6 = f32[4,60,256]{2,1,0:T(8,128)S(1)} fusion(f32[60,35,1]{0,1,2:T(8,128)} %constant.129, f32[4,35,256]{2,0,1:T(4,128)} %param.14), kind=kOutput, calls=%fused_computation.14 | convolution fusion | flops 25804800 | bytes 397520 | tf_op jit(solution)/shard_map/kn,cne->cke/dot_general | solution.py:171
  6.0 3.3 %scatter_custom_fusion = f32[1600,60]{1,0:T(8,128)S(1)} fusion(s32[1024]{0:T(1024)S(1)} %broadcast_select_fusion, f32[1024,60]{1,0:T(8,128)S(1)} %copy.100, f32[]{:T(128)} %constant.36.clone.1), kind=kCustom, calls=%fused_computation.21 | custom fusion | bytes 384004
  9.3 0.6 slice_bitcast_fusion.1
  9.9 1.9 %collective-permute-start = (f32[60,32]{0,1:T(8,128)}, f32[60,32]{0,1:T(8,128)}, u32[]{:S(2)}, u32[]{:S(2)}) collective-permute-start(f32[60,32]{0,1:T(8,128)} %get-tuple-element.21), channel_id=1, source_target_pairs={{0,48},{48,96},{96,144},{144,192},{192,240},{240,288},{288,336},{3... | collective-permute-start | bytes 23048 | tf_op jit(solution)/shard_map/ppermute | solution.py:23
  11.8 3.8 %collective-permute-start.1 = (f32[60,32]{0,1:T(8,128)}, f32[60,32]{0,1:T(8,128)}, u32[]{:S(2)}, u32[]{:S(2)}) collective-permute-start(f32[60,32]{0,1:T(8,128)} %get-tuple-element.22), channel_id=1, source_target_pairs={{48,0},{96,48},{144,96},{192,144},{240,192},{288,240},{336,288},{3... | collective-permute-start | bytes 23048 | tf_op jit(solution)/shard_map/ppermute | solution.py:23
  15.6 2.0 %reshape.426 = f32[48,1,1920]{2,1,0:T(1,128)} reshape(f32[48,32,60]{2,1,0:T(8,128)S(1)} %slice_bitcast_fusion.2) | data formatting | bytes 737280
  17.6 18.6 %all-to-all-start = ((f32[48,1,1920]{2,1,0:T(1,128)}), f32[48,1,1920]{2,1,0:T(1,128)}, u32[]{:S(2)}, u32[]{:S(2)}) async-start(f32[48,1,1920]{2,1,0:T(1,128)} %reshape.426), calls=%async_computation | async-start | bytes 737280 | tf_op jit(solution)/shard_map/all_to_all | solution.py:184
  37.5 0.6 broadcast_compare_fusion.5
  38.2 0.6 broadcast_multiply_fusion.1
  38.9 0.6 bitcast_multiply_fusion
  40.0 1.4 %copy.96 = f32[3,4,35,256]{2,0,1,3:T(4,128)S(1)} copy(f32[3,4,35,256]{3,2,0,1:T(8,128)S(1)} %convolution_bitcast_fusion) | data formatting | bytes 860160 | tf_op jit(solution)/shard_map/dnm,cme->dcne/transpose | solution.py:137
  41.4 0.6 reshape.384
  42.0 0.9 copy.95
  43.0 5.7 %fusion.5 = f32[256,4,35,3]{2,3,1,0:T(4,128)} fusion(f32[3,4,35,256]{2,0,1,3:T(4,128)S(1)} %copy.96, f32[3,3,256]{1,0,2:T(4,128)S(1)} %copy.95, f32[256]{0:T(256)} %copy-done.9), kind=kOutput, calls=%fused_computation.17 | convolution fusion | flops 3873024 | bytes 870400 | tf_op jit(solution)/shard_map/ide,dcne->icne/dot_general | solution.py:139
  48.8 2.0 %copy.97 = f32[256,4,35,3]{0,3,2,1:T(4,128)S(1)} copy(f32[256,4,35,3]{2,3,1,0:T(4,128)} %fusion.5) | data formatting | bytes 860160 | tf_op jit(solution)/shard_map/ide,dcne->icne/dot_general | solution.py:139
  52.3 2.8 %gather_fusion = f32[1024,60]{1,0:T(8,128)S(1)} fusion(f32[60,1024]{0,1:T(8,128)S(1)} %copy.99, s32[1024]{0:T(1024)S(1)} %broadcast_clamp_fusion), kind=kCustom, calls=%fused_computation | custom fusion | bytes 495616 | tf_op jit(solution)/shard_map/jit(_take)/gather | solution.py:189
  55.1 1.1 all-to-all-done
  56.7 2.5 %reduce.5 = f32[48,1920]{1,0:T(8,128)S(1)} reduce(f32[48,1,1920]{2,1,0:T(1,128)} %all-to-all-done, f32[]{:T(128)} %broadcast.470), dimensions={1}, to_apply=%all_to_all.3.reduce_sub_computation | reduce | bytes 737284 | tf_op jit(solution)/shard_map/all_to_all | solution.py:184
  59.2 1.2 reshape.427
  60.4 0.8 pad_maximum_fusion
  61.2 6.8 %gather_fusion.1 = f32[1024,60]{1,0:T(8,128)S(1)} fusion(f32[50,60,32]{1,2,0:T(8,128)S(1)} %pad_maximum_fusion, s32[1024]{0:T(1024)S(1)} %bitcast.111), kind=kCustom, calls=%fused_computation.1 | custom fusion | bytes 499712 | tf_op jit(solution)/shard_map/gather | solution.py:190
  68.0 0.8 select_bitcast_fusion
  71.7 0.9 multiply_reduce_fusion.1
  72.6 0.6 multiply_reduce_fusion.3
  73.2 16.3 %psum.28 = f32[]{:T(128)} all-reduce(f32[]{:T(128)} %multiply_reduce_fusion.3), channel_id=1, replica_groups=mesh['grp_0'=8,'grp_1'=2,'sub_0'=12,'sub_1'=4] {'grp_0'}, use_global_device_ids=true, to_apply=%region_5.6 | all-reduce | flops 1 | bytes 8 | tf_op jit(solution)/shard_map/psum | solution.py:28
  89.5 3.1 %psum.29 = f32[]{:T(128)} all-reduce(f32[]{:T(128)} %psum.28), channel_id=1, replica_groups=mesh['grp_0'=8,'grp_1'=2,'sub_0'=12,'sub_1'=4] {'grp_1'}, use_global_device_ids=true, to_apply=%region_6.7 | all-reduce | flops 1 | bytes 8 | tf_op jit(solution)/shard_map/psum | solution.py:28
  92.6 24.5 %psum.30 = f32[]{:T(128)} all-reduce(f32[]{:T(128)} %psum.29), channel_id=1, replica_groups=mesh['grp_0'=8,'grp_1'=2,'sub_0'=12,'sub_1'=4] {'sub_0'}, use_global_device_ids=true, to_apply=%region_7.8 | all-reduce | flops 1 | bytes 8 | tf_op jit(solution)/shard_map/psum | solution.py:28
  117.1 11.0 %psum.31 = f32[]{:T(128)} all-reduce(f32[]{:T(128)} %psum.30), channel_id=1, replica_groups=mesh['grp_0'=8,'grp_1'=2,'sub_0'=12,'sub_1'=4] {'sub_1'}, use_global_device_ids=true, to_apply=%region_8.9 | all-reduce | flops 1 | bytes 8 | tf_op jit(solution)/shard_map/psum | solution.py:28
  (124 shorter events, 6.8 us)
Async XLA Ops:
  0.6 38.8 %copy-start = (f32[3,35,35]{2,1,0:T(8,128)S(1)}, f32[3,35,35]{2,1,0:T(8,128)}, u32[]{:S(2)}) copy-start(f32[3,35,35]{2,1,0:T(8,128)} %param.24) | copy-start | bytes 44104
  5.9 30.4 %copy-start.32 = (s32[256]{0:T(256)S(1)}, s32[256]{0:T(256)}, u32[]{:S(2)}) copy-start(s32[256]{0:T(256)} %param.21) | copy-start | bytes 3076
  5.9 30.4 %copy-start.12 = (f32[4,256]{1,0:T(4,128)S(1)}, f32[4,256]{1,0:T(4,128)}, u32[]{:S(2)}) copy-start(f32[4,256]{1,0:T(4,128)} %param.18) | copy-start | bytes 12292
  5.9 31.6 %copy-start.28 = (s32[4,256]{1,0:T(4,128)S(1)}, s32[4,256]{1,0:T(4,128)}, u32[]{:S(2)}) copy-start(s32[4,256]{1,0:T(4,128)} %param.23) | copy-start | bytes 12292
  5.9 32.2 %copy-start.7 = (f32[4,3,256]{2,0,1:T(4,128)S(1)}, f32[4,3,256]{2,0,1:T(4,128)}, u32[]{:S(2)}) copy-start(f32[4,3,256]{2,0,1:T(4,128)} %param.17) | copy-start | bytes 36868
  9.9 50.5 %collective-permute-start = (f32[60,32]{0,1:T(8,128)}, f32[60,32]{0,1:T(8,128)}, u32[]{:S(2)}, u32[]{:S(2)}) collective-permute-start(f32[60,32]{0,1:T(8,128)} %get-tuple-element.21), channel_id=1, source_target_pairs={{0,48},{48,96},{96,144},{144,192},{192,240},{240,288},{288,336},{3... | collective-permute-start | bytes 23048 | tf_op jit(solution)/shard_map/ppermute | solution.py:23
  11.8 27.7 %copy-start.1 = (f32[4,35,256]{2,0,1:T(4,128)S(1)}, f32[4,35,256]{2,0,1:T(4,128)}, u32[]{:S(2)}) copy-start(f32[4,35,256]{2,0,1:T(4,128)} %param.14) | copy-start | bytes 430084
  11.8 48.6 %collective-permute-start.1 = (f32[60,32]{0,1:T(8,128)}, f32[60,32]{0,1:T(8,128)}, u32[]{:S(2)}, u32[]{:S(2)}) collective-permute-start(f32[60,32]{0,1:T(8,128)} %get-tuple-element.22), channel_id=1, source_target_pairs={{48,0},{96,48},{144,96},{192,144},{240,192},{288,240},{336,288},{3... | collective-permute-start | bytes 23048 | tf_op jit(solution)/shard_map/ppermute | solution.py:23
  17.6 38.6 %all-to-all-start = ((f32[48,1,1920]{2,1,0:T(1,128)}), f32[48,1,1920]{2,1,0:T(1,128)}, u32[]{:S(2)}, u32[]{:S(2)}) async-start(f32[48,1,1920]{2,1,0:T(1,128)} %reshape.426), calls=%async_computation | async-start | bytes 737280 | tf_op jit(solution)/shard_map/all_to_all | solution.py:184
  36.3 5.1 %copy-start.10 = (f32[9,256]{1,0:T(8,128)S(1)}, f32[9,256]{1,0:T(8,128)}, u32[]{:S(2)}) copy-start(f32[9,256]{1,0:T(8,128)} %param.16) | copy-start | bytes 27652
  36.3 1.9 %copy-start.9 = (f32[256]{0:T(256)}, f32[256]{0:T(256)S(1)}, u32[]{:S(2)}) copy-start(f32[256]{0:T(256)S(1)} %multiply_exponential_fusion) | copy-start | bytes 3076
  48.7 2.1 %copy-start.11 = (s32[1,2,4,128]{3,1,2,0:T(2,128)S(1)}, s32[1,2,4,128]{3,1,2,0:T(2,128)}, u32[]{:S(2)}) copy-start(s32[1,2,4,128]{3,1,2,0:T(2,128)} %copy.113) | copy-start | bytes 12292
  48.7 2.9 %copy-start.30 = (f32[256]{0:T(256)S(1)}, f32[256]{0:T(256)}, u32[]{:S(2)}) copy-start(f32[256]{0:T(256)} %param.19) | copy-start | bytes 3076
  48.7 2.9 %copy-start.31 = (s32[256]{0:T(256)S(1)}, s32[256]{0:T(256)}, u32[]{:S(2)}) copy-start(s32[256]{0:T(256)} %param.20) | copy-start | bytes 3076
  48.7 3.1 %copy-start.15 = (pred[4,256]{1,0:T(4,128)(4,1)S(1)}, pred[4,256]{1,0:T(4,128)(4,1)}, u32[]{:S(2)}) copy-start(pred[4,256]{1,0:T(4,128)(4,1)} %copy-done.14) | copy-start | bytes 3076
  48.7 3.1 %copy-start.22 = (pred[4,256]{1,0:T(4,128)(4,1)S(1)}, pred[4,256]{1,0:T(4,128)(4,1)}, u32[]{:S(2)}) copy-start(pred[4,256]{1,0:T(4,128)(4,1)} %get-tuple-element.28) | copy-start | bytes 3076
  48.7 3.1 %copy-start.27 = (pred[4,256]{1,0:T(4,128)(4,1)S(1)}, pred[4,256]{1,0:T(4,128)(4,1)}, u32[]{:S(2)}) copy-start(pred[4,256]{1,0:T(4,128)(4,1)} %get-tuple-element.31) | copy-start | bytes 3076
  48.7 3.2 %copy-start.26 = (pred[4,256]{1,0:T(4,128)(4,1)S(1)}, pred[4,256]{1,0:T(4,128)(4,1)}, u32[]{:S(2)}) copy-start(pred[4,256]{1,0:T(4,128)(4,1)} %get-tuple-element.34) | copy-start | bytes 3076
  48.8 3.2 %copy-start.25 = (pred[4,256]{1,0:T(4,128)(4,1)S(1)}, pred[4,256]{1,0:T(4,128)(4,1)}, u32[]{:S(2)}) copy-start(pred[4,256]{1,0:T(4,128)(4,1)} %get-tuple-element.33) | copy-start | bytes 3076
  48.8 3.2 %copy-start.24 = (pred[4,256]{1,0:T(4,128)(4,1)S(1)}, pred[4,256]{1,0:T(4,128)(4,1)}, u32[]{:S(2)}) copy-start(pred[4,256]{1,0:T(4,128)(4,1)} %get-tuple-element.30) | copy-start | bytes 3076
  48.8 3.2 %copy-start.23 = (pred[4,256]{1,0:T(4,128)(4,1)S(1)}, pred[4,256]{1,0:T(4,128)(4,1)}, u32[]{:S(2)}) copy-start(pred[4,256]{1,0:T(4,128)(4,1)} %get-tuple-element.32) | copy-start | bytes 3076
  48.8 3.3 %copy-start.21 = (pred[4,256]{1,0:T(4,128)(4,1)S(1)}, pred[4,256]{1,0:T(4,128)(4,1)}, u32[]{:S(2)}) copy-start(pred[4,256]{1,0:T(4,128)(4,1)} %get-tuple-element.27) | copy-start | bytes 3076
  48.8 3.3 %copy-start.13 = (f32[1,2,4,128]{3,2,1,0:T(4,128)S(1)}, f32[1,2,4,128]{3,2,1,0:T(4,128)}, u32[]{:S(2)}) copy-start(f32[1,2,4,128]{3,2,1,0:T(4,128)} %fusion.47) | copy-start | bytes 12292
  48.8 3.4 %copy-start.8 = (f32[35,60]{1,0:T(8,128)S(1)}, f32[35,60]{1,0:T(8,128)}, u32[]{:S(2)}) copy-start(f32[35,60]{1,0:T(8,128)} %param.25) | copy-start | bytes 25204
  61.2 6.8 %copy-start.29 = (pred[1024]{0:T(1024)(128)(4,1)S(1)}, pred[1024]{0:T(1024)(128)(4,1)}, u32[]{:S(2)}) copy-start(pred[1024]{0:T(1024)(128)(4,1)} %compare_and_fusion) | copy-start | bytes 3076
  68.0 1.5 %copy-start.19 = (f32[15,15,1]{1,0,2:T(8,128)S(1)}, f32[15,15,1]{1,0,2:T(8,128)}, u32[]{:S(2)}) copy-start(f32[15,15,1]{1,0,2:T(8,128)} %constant.132) | copy-start | bytes 2704
  68.0 1.9 %copy-start.18 = (f32[15,15,1]{1,0,2:T(8,128)S(1)}, f32[15,15,1]{1,0,2:T(8,128)}, u32[]{:S(2)}) copy-start(f32[15,15,1]{1,0,2:T(8,128)} %constant.130) | copy-start | bytes 2704
  68.0 2.3 %copy-start.17 = (f32[15,15,1]{1,0,2:T(8,128)S(1)}, f32[15,15,1]{1,0,2:T(8,128)}, u32[]{:S(2)}) copy-start(f32[15,15,1]{1,0,2:T(8,128)} %constant.134) | copy-start | bytes 2704
  68.9 1.8 %copy-start.16 = (f32[15,15,1]{1,0,2:T(8,128)S(1)}, f32[15,15,1]{1,0,2:T(8,128)}, u32[]{:S(2)}) copy-start(f32[15,15,1]{1,0,2:T(8,128)} %constant.131) | copy-start | bytes 2704
  69.1 2.0 %copy-start.3 = (f32[1,3,4,256]{3,1,2,0:T(4,128)S(1)}, f32[1,3,4,256]{3,1,2,0:T(4,128)}, u32[]{:S(2)}) copy-start(f32[1,3,4,256]{3,1,2,0:T(4,128)} %copy-done.2) | copy-start | bytes 36868
  69.1 2.0 %copy-start.5 = (f32[3,1024]{1,0:T(4,128)S(1)}, f32[3,1024]{1,0:T(4,128)}, u32[]{:S(2)}) copy-start(f32[3,1024]{1,0:T(4,128)} %broadcast_multiply_fusion.1) | copy-start | bytes 36868
  70.3 1.4 %copy-start.4 = (f32[4,35,256]{2,0,1:T(4,128)S(1)}, f32[4,35,256]{2,0,1:T(4,128)}, u32[]{:S(2)}) copy-start(f32[4,35,256]{2,0,1:T(4,128)} %param.15) | copy-start | bytes 430084
  (4 other events, 4.6 us)
where the time goes:
time: 131 us; the launch traced here: 130 us
  blocking collectives  54.9 us (42%)
  starting transfers between devices  24.3 us (19%)
  local copies, waits for them, and re-layouts  24.1 us (18%)
  other arithmetic  12.5 us (10%)
  matrix products  9.78 us (7%)
  between operations  3.28 us (3%)
    psum x4, blocking collectives, by_axis(): value = lax.psum(value, axis)  54.9 us
    all_to_all x1, starting transfers between devices, local(): lax.all_to_all(outbox[:peer_count], SUB, split_axis=0, concat_axis=0, til...  18.6 us
    unnamed x77, local copies, waits for them, and re-layouts  7.35 us
    gather x1, local copies, waits for them, and re-layouts, local(): far_pick = received[jnp.minimum(block_index, block_total - 1), :, within].T  6.79 us
    dot_general x1, matrix products, advance(): jnp.einsum('ide,dcne->icne', metric, slopes, precision=lax.Precision.HIGH...  5.75 us
    ppermute x2, starting transfers between devices, passed_along(): lax.ppermute(value, axis, [(source, source + steps) for source in range(f...  5.69 us
    gather x1, local copies, waits for them, and re-layouts, local(): jnp.take(inner_cols, jnp.clip(face_codes, 0, total_faces - 1), axis=1)  2.81 us
    unnamed x5, other arithmetic  2.78 us
  transfers between devices with their start and end apart: 3, of which 1 were waited for; matrix products, arithmetic and copies ran while one was open for 19% of the time, Pallas kernels for 0%

commit v1 on v0

v1 whole, which is shorter than its diff:
```python
import functools

import jax
import jax.numpy as jnp
import numpy as np
from jax import lax
from jax.experimental import pallas as pl
from jax.experimental.pallas import tpu as pltpu
from jax.sharding import PartitionSpec as P

MESH = pl.DeviceIdType.MESH
F32 = jnp.float32
BF16 = jnp.bfloat16

RUNGE_CARRY = -567301805773.0 / 1357537059087.0
RUNGE_ADVANCE = 5161836677717.0 / 13612068292357.0
TIME_STEP = 0.02

NODES = 35
ELEMS = 256
FACES = 4 * ELEMS
NEAR = 4
NEAR_ROWS = 9 * 16
RING = 4


def pick_table():
    volume = [(a, b, c, 4 - a - b - c) for a in range(5) for b in range(5 - a) for c in range(5 - a - b)]
    triples = [(a, b, 4 - a - b) for a in range(5) for b in range(5 - a)]
    orders = [(0, 1, 2), (1, 2, 0), (2, 0, 1), (0, 2, 1), (2, 1, 0), (1, 0, 2)]
    inverse = [0, 2, 1, 3, 4, 5]
    table = np.zeros((4, 6, 16, 2, 48), np.float32)
    for facet in range(4):
        others = [corner for corner in range(4) if corner != facet]
        for option in range(6):
            order = orders[inverse[option]]
            for node in range(15):
                triple = triples[node]
                turned = tuple(triple[q] for q in order)
                corners = [0, 0, 0, 0]
                for place in range(3):
                    corners[others[place]] = turned[place]
                table[facet, option, node, :, volume.index(tuple(corners))] = 1.0
    return table.reshape(4, 96, 96)


def split(value):
    high = value.astype(BF16)
    low = (value - high.astype(F32)).astype(BF16)
    return high, low


def kernel(
    ng,
    ns,
    half,
    fields,
    store,
    metric,
    normals,
    scale,
    damping,
    mask,
    level,
    source,
    orient,
    deriv,
    lift,
    picks,
    fields_out,
    store_out,
    energy_out,
    stacked,
    inner,
    turned,
    place,
    local,
    base,
    lifts,
    near_box,
    far_box,
    grp_box,
    near_in,
    far_in,
    grp_in,
    stage,
    row_own,
    row_sub,
    sum_own,
    row_grp,
    send_sem,
    recv_sem,
    grp_send,
    grp_recv,
    esend_sub,
    erecv_sub,
    esend_grp,
    erecv_grp,
):
    g = lax.axis_index("grp")
    s = lax.axis_index("sub")
    nz = ns // RING
    far_at = NEAR_ROWS
    grp_at = NEAR_ROWS + 4 * ns
    rows = grp_at + 32

    def peer_of(m):
        i = m // RING
        j = RING - 1 - m % RING
        off = nz // 2 + (1 - 2 * (i % 2)) * ((i + 1) // 2)
        z = (s // RING + off) % nz
        x = (s % RING + j) % RING
        return z * RING + x

    near_in[...] = jnp.zeros_like(near_in)
    far_in[...] = jnp.zeros_like(far_in)
    grp_in[...] = jnp.zeros_like(grp_in)

    barrier = pltpu.get_barrier_semaphore()

    def greet_sub(m, carry):
        pl.semaphore_signal(barrier, inc=1, device_id=(g, peer_of(m)), device_id_type=MESH)
        return carry

    def greet_grp(k, carry):
        pl.semaphore_signal(barrier, inc=1, device_id=((g + k) % ng, s), device_id_type=MESH)
        return carry

    lax.fori_loop(0, ns - 1, greet_sub, 0)
    lax.fori_loop(1, ng, greet_grp, 0)

    stacked[...] = jnp.zeros_like(stacked)
    for c in range(4):
        high, low = split(fields[c])
        stacked[c, 0:NODES, :] = high
        stacked[c, 48 : 48 + NODES, :] = low
    for f in range(4):
        option_of = orient[f : f + 1, :]
        at = slice(f * ELEMS, (f + 1) * ELEMS)
        for c in range(4):
            found = jnp.dot(picks[f], stacked[c], preferred_element_type=F32)
            inner[c * 16 : (c + 1) * 16, at] = found[0:16]
            chosen = found[0:16]
            for option in range(1, 6):
                chosen = jnp.where(option_of == option, found[option * 16 : (option + 1) * 16], chosen)
            high, low = split(chosen)
            turned[c * 16 : (c + 1) * 16, at] = high
            turned[64 + c * 16 : 64 + (c + 1) * 16, at] = low

    codes = jnp.concatenate([source[f : f + 1, :] for f in range(4)], axis=1)
    slot = codes - FACES
    block = slot >> 5
    rank = slot & 31
    delta = block - s
    beside = (block < ns) & (delta >= -NEAR) & (delta <= NEAR)
    apart = (block < ns) & jnp.logical_not(beside)
    row = jnp.where(
        apart,
        far_at + block * 4 + (rank & 3),
        jnp.where(beside, (delta + NEAR) * 16, grp_at + (block - ns) * 16) + (rank & 15),
    )
    row = row + half * jnp.where(apart, (rank >> 2) & 1, rank >> 4)
    row = jnp.where(codes >= FACES, row, -1)

    def build_place(i, carry):
        at = lax.broadcasted_iota(jnp.int32, (32, FACES), 0) + i * 32
        place[pl.ds(i * 32, 32), :] = jnp.where(at == row, 1.0, 0.0).astype(BF16)
        return carry

    lax.fori_loop(0, 2 * half // 32, build_place, 0)

    packed = lax.dot_general(place[...], turned[...], (((1,), (1,)), ((), ())), preferred_element_type=F32)
    left, right = packed[:half], packed[half:]
    left = left + pltpu.roll(left, 64, 1)
    right = right + pltpu.roll(right, 64, 1)
    lane = lax.broadcasted_iota(jnp.int32, (half, 128), 1)
    out = jnp.where(lane < 64, left, right)
    near_box[...] = out[:far_at].reshape(9, 16, 128)
    for b in range(ns):
        far_box[b] = out[far_at + 4 * b : far_at + 4 * b + 4]
    grp_box[...] = out[grp_at:rows].reshape(2, 16, 128)

    pl.semaphore_wait(barrier, ns - 1 + ng - 1)

    def near_copy(b):
        return pltpu.make_async_remote_copy(
            src_ref=near_box.at[b - s + NEAR],
            dst_ref=near_in.at[s - b + NEAR],
            send_sem=send_sem.at[b],
            recv_sem=recv_sem.at[s],
            device_id=(g, b),
            device_id_type=MESH,
        )

    def far_copy(b):
        return pltpu.make_async_remote_copy(
            src_ref=far_box.at[b],
            dst_ref=far_in.at[s],
            send_sem=send_sem.at[b],
            recv_sem=recv_sem.at[s],
            device_id=(g, b),
            device_id_type=MESH,
        )

    def near_arrival(b):
        return pltpu.make_async_remote_copy(
            src_ref=near_box.at[b - s + NEAR],
            dst_ref=near_in.at[b - s + NEAR],
            send_sem=send_sem.at[b],
            recv_sem=recv_sem.at[b],
            device_id=(g, b),
            device_id_type=MESH,
        )

    def far_arrival(b):
        return pltpu.make_async_remote_copy(
            src_ref=far_box.at[b],
            dst_ref=far_in.at[b],
            send_sem=send_sem.at[b],
            recv_sem=recv_sem.at[b],
            device_id=(g, b),
            device_id_type=MESH,
        )

    def is_near(b):
        return (b - s <= NEAR) & (s - b <= NEAR)

    def grp_copy(up):
        return pltpu.make_async_remote_copy(
            src_ref=grp_box.at[up],
            dst_ref=grp_in.at[1 - up],
            send_sem=grp_send.at[up],
            recv_sem=grp_recv.at[1 - up],
            device_id=(g + 2 * up - 1, s),
            device_id_type=MESH,
        )

    def send_sub(m, carry):
        b = peer_of(m)

        @pl.when(is_near(b))
        def _():
            near_copy(b).start()

        @pl.when(jnp.logical_not(is_near(b)))
        def _():
            far_copy(b).start()

        return carry

    lax.fori_loop(0, ns - 1, send_sub, 0)

    @pl.when(g < ng - 1)
    def _():
        grp_copy(1).start()

    @pl.when(g > 0)
    def _():
        grp_copy(0).start()

    growth = jnp.exp2(level[...].astype(F32))
    absorb = damping[...] * mask[...].astype(F32)

    def build_local(i, carry):
        at = lax.broadcasted_iota(jnp.int32, (32, FACES), 0) + i * 32
        local[pl.ds(i * 32, 32), :] = jnp.where(at == codes, 1.0, 0.0).astype(BF16)
        return carry

    lax.fori_loop(0, FACES // 32, build_local, 0)
    outer_own = jnp.dot(turned[...], local[...], preferred_element_type=F32)

    lifts[...] = jnp.zeros_like(lifts)
    for f in range(4):
        lifts[0:NODES, f * 16 : f * 16 + 15] = lift[:, f * 15 : (f + 1) * 15]

    slopes = [
        [jnp.dot(deriv[d], fields[c], precision=lax.Precision.HIGHEST, preferred_element_type=F32) for c in range(4)]
        for d in range(3)
    ]

    def physical(x, c):
        total = metric[3 * x : 3 * x + 1, :] * slopes[0][c]
        for y in range(1, 3):
            total = total + metric[3 * x + y : 3 * x + y + 1, :] * slopes[y][c]
        return growth * total

    volume = [-(physical(0, 1) + physical(1, 2) + physical(2, 3))]
    volume += [-physical(x, 0) for x in range(3)]
    for c in range(4):
        base[c] = RUNGE_CARRY * store[c] + TIME_STEP * (volume[c] - absorb * fields[c])

    def arrive(m, carry):
        b = peer_of(m)

        @pl.when(is_near(b))
        def _():
            near_arrival(b).wait_recv()

        @pl.when(jnp.logical_not(is_near(b)))
        def _():
            far_arrival(b).wait_recv()

        return carry

    lax.fori_loop(0, ns - 1, arrive, 0)

    def grp_arrival(down):
        return pltpu.make_async_remote_copy(
            src_ref=grp_box.at[down],
            dst_ref=grp_in.at[down],
            send_sem=grp_send.at[down],
            recv_sem=grp_recv.at[down],
            device_id=(g + 2 * down - 1, s),
            device_id_type=MESH,
        )

    @pl.when(g > 0)
    def _():
        grp_arrival(0).wait_recv()

    @pl.when(g < ng - 1)
    def _():
        grp_arrival(1).wait_recv()

    stage[0:far_at, :] = near_in[...].reshape(far_at, 128)
    for b in range(ns):
        stage[far_at + 4 * b : far_at + 4 * b + 4, :] = far_in[b]
    stage[grp_at:rows, :] = grp_in[...].reshape(32, 128)
    if half > rows:
        stage[rows:half, :] = jnp.zeros((half - rows, 128), F32)
    came = stage[...].T
    came_high, came_low = split(came)
    left = jnp.concatenate([came_high[0:64], came_low[0:64]], axis=0)
    right = jnp.concatenate([came_high[64:128], came_low[64:128]], axis=0)
    outer_all = (
        outer_own
        + jnp.dot(left, place[0:half, :], preferred_element_type=F32)
        + jnp.dot(right, place[half : 2 * half, :], preferred_element_type=F32)
    )
    outer = outer_all[0:64] + outer_all[64:128]

    flux = [[None] * 4 for _ in range(4)]
    for f in range(4):
        at = slice(f * ELEMS, (f + 1) * ELEMS)
        wall = source[f : f + 1, :] < 0
        norm = [normals[f, x : x + 1, :] for x in range(3)]
        press_in = inner[0:16, at]
        veloc_in = [inner[(1 + x) * 16 : (2 + x) * 16, at] for x in range(3)]
        along = norm[0] * veloc_in[0] + norm[1] * veloc_in[1] + norm[2] * veloc_in[2]
        press_jump = jnp.where(wall, 0.0, press_in - outer[0:16, at])
        normal_jump = jnp.zeros_like(along)
        for x in range(3):
            met = jnp.where(wall, veloc_in[x] - 2.0 * norm[x] * along, outer[(1 + x) * 16 : (2 + x) * 16, at])
            normal_jump = normal_jump + norm[x] * (veloc_in[x] - met)
        weight = 0.5 * scale[f : f + 1, :] * growth
        flux[0][f] = weight * (normal_jump - press_jump)
        for x in range(3):
            flux[1 + x][f] = -norm[x] * flux[0][f]

    energy = jnp.zeros((1, ELEMS), F32)
    for c in range(4):
        lifted = jnp.dot(
            lifts[0:40, :],
            jnp.concatenate(flux[c], axis=0),
            precision=lax.Precision.HIGHEST,
            preferred_element_type=F32,
        )
        store_next = base[c] + TIME_STEP * lifted[0:NODES]
        fields_next = fields[c] + RUNGE_ADVANCE * store_next
        store_out[c] = store_next
        fields_out[c] = fields_next
        energy = energy + jnp.sum(fields_next * fields_next, axis=0, keepdims=True)
    energy = absorb * energy
    row_own[...] = energy[:, 0:128] + energy[:, 128:256]

    def sub_row(b, at):
        return pltpu.make_async_remote_copy(
            src_ref=row_own,
            dst_ref=row_sub.at[at],
            send_sem=esend_sub.at[b],
            recv_sem=erecv_sub.at[at],
            device_id=(g, b),
            device_id_type=MESH,
        )

    def send_row(m, carry):
        sub_row(peer_of(m), s).start()
        return carry

    lax.fori_loop(0, ns - 1, send_row, 0)
    row_sub[s] = row_own[...]

    def take_row(m, carry):
        b = peer_of(m)
        sub_row(b, b).wait_recv()
        return carry

    lax.fori_loop(0, ns - 1, take_row, 0)
    sum_own[...] = jnp.sum(row_sub[...], axis=0)

    def grp_row(b, at):
        return pltpu.make_async_remote_copy(
            src_ref=sum_own,
            dst_ref=row_grp.at[at],
            send_sem=esend_grp.at[b],
            recv_sem=erecv_grp.at[at],
            device_id=(b, s),
            device_id_type=MESH,
        )

    def send_sum(k, carry):
        grp_row((g + k) % ng, g).start()
        return carry

    lax.fori_loop(1, ng, send_sum, 0)
    row_grp[g] = sum_own[...]

    def sent_sub(m, carry):
        b = peer_of(m)

        @pl.when(is_near(b))
        def _():
            near_copy(b).wait_send()

        @pl.when(jnp.logical_not(is_near(b)))
        def _():
            far_copy(b).wait_send()

        sub_row(b, s).wait_send()
        return carry

    lax.fori_loop(0, ns - 1, sent_sub, 0)

    @pl.when(g < ng - 1)
    def _():
        grp_copy(1).wait_send()

    @pl.when(g > 0)
    def _():
        grp_copy(0).wait_send()

    def take_sum(k, carry):
        b = (g + k) % ng
        grp_row(b, b).wait_recv()
        return carry

    lax.fori_loop(1, ng, take_sum, 0)
    total = jnp.sum(jnp.sum(row_grp[...], axis=0))
    energy_out[0, 0] = total * (1.0 / (ELEMS * NODES * ng * ns))

    def sent_sum(k, carry):
        grp_row((g + k) % ng, g).wait_send()
        return carry

    lax.fori_loop(1, ng, sent_sum, 0)


def solution(mesh):
    ng, ns = mesh.shape["grp"], mesh.shape["sub"]
    rows = NEAR_ROWS + 4 * ns + 32
    half = -(-rows // 128) * 128
    both = ("grp", "sub")
    vmem = pl.BlockSpec(memory_space=pltpu.VMEM)
    dma = pltpu.SemaphoreType.DMA

    call = pl.pallas_call(
        functools.partial(kernel, ng, ns, half),
        out_shape=(
            jax.ShapeDtypeStruct((4, NODES, ELEMS), F32),
            jax.ShapeDtypeStruct((4, NODES, ELEMS), F32),
            jax.ShapeDtypeStruct((1, 1), F32),
        ),
        in_specs=[vmem] * 13,
        out_specs=(vmem, vmem, pl.BlockSpec(memory_space=pltpu.SMEM)),
        scratch_shapes=[
            pltpu.VMEM((4, 96, ELEMS), BF16),
            pltpu.VMEM((64, FACES), F32),
            pltpu.VMEM((128, FACES), BF16),
            pltpu.VMEM((2 * half, FACES), BF16),
            pltpu.VMEM((FACES, FACES), BF16),
            pltpu.VMEM((4, NODES, ELEMS), F32),
            pltpu.VMEM((40, 64), F32),
            pltpu.VMEM((9, 16, 128), F32),
            pltpu.VMEM((ns, 4, 128), F32),
            pltpu.VMEM((2, 16, 128), F32),
            pltpu.VMEM((9, 16, 128), F32),
            pltpu.VMEM((ns, 4, 128), F32),
            pltpu.VMEM((2, 16, 128), F32),
            pltpu.VMEM((half, 128), F32),
            pltpu.VMEM((1, 128), F32),
            pltpu.VMEM((ns, 1, 128), F32),
            pltpu.VMEM((1, 128), F32),
            pltpu.VMEM((ng, 1, 128), F32),
            dma((ns,)),
            dma((ns,)),
            dma((2,)),
            dma((2,)),
            dma((ns,)),
            dma((ns,)),
            dma((ng,)),
            dma((ng,)),
        ],
        compiler_params=pltpu.CompilerParams(collective_id=0, has_side_effects=True),
        name="section",
    )

    def local(
        fields,
        section_store,
        metric_terms,
        normals,
        face_scale,
        damping,
        absorb_mask,
        refine_level,
        face_source,
        orientation,
        derivative,
        lift_matrix,
    ):
        fields_next, store_next, energy = call(
            fields,
            section_store,
            metric_terms,
            normals,
            face_scale,
            damping.reshape(1, ELEMS),
            absorb_mask.reshape(1, ELEMS),
            refine_level.reshape(1, ELEMS),
            face_source,
            orientation,
            derivative,
            lift_matrix,
            jnp.asarray(pick_table(), BF16),
        )
        return fields_next, store_next, energy.reshape(())

    in_specs = (
        P(None, None, both),
        P(None, None, both),
        P(None, both),
        P(None, None, both),
        P(None, both),
        P(both),
        P(both),
        P(both),
        P(None, both),
        P(None, both),
        P(),
        P(),
    )
    out_specs = (P(None, None, both), P(None, None, both), P())
    return jax.shard_map(local, mesh=mesh, in_specs=in_specs, out_specs=out_specs, check_vma=False)
```

time: 131 us -> 56.9 us (0.43)
  the two profiles are of different devices: /device:TPU:40 before, /device:TPU:1 now
where the time goes in v1:
time: 56.9 us; the launch traced here: 56.6 us
  Pallas kernels  48.2 us (85%)
  local copies, waits for them, and re-layouts  6.04 us (11%)
  between operations  2.36 us (4%)
    pallas_call x1, Pallas kernels, local(): call(fields, section_store, metric_terms, normals, face_scale, damping.re...  48.2 us
    unnamed x9, local copies, waits for them, and re-layouts  6.04 us

profile of v1, /device:TPU:1, one launch (start us, length us, event | category | flops | bytes accessed | tf_op | source)
XLA Modules:
  0.0 56.6 jit_solution(14991878762982112057)
XLA Ops:
  0.6 1.3 %copy.18.normals = f32[4,3,256]{2,1,0:T(4,128)} copy(f32[4,3,256]{2,0,1:T(4,128)} %param.16) | data formatting | bytes 24576 | tf_op args[3]
  1.9 0.0 copy-start.1
  1.9 1.6 %copy.16.fields = f32[4,35,256]{2,1,0:T(8,128)} copy(f32[4,35,256]{2,0,1:T(4,128)} %param.13) | data formatting | bytes 286720 | tf_op args[0]
  3.6 0.0 copy-done.1
  3.6 0.7 %copy.17.store = f32[4,35,256]{2,1,0:T(8,128)} copy(f32[4,35,256]{2,0,1:T(4,128)S(1)} %copy-done.1) | data formatting | bytes 286720 | tf_op args[1]
  4.3 48.2 %section.1 = (f32[4,35,256]{2,1,0:T(8,128)}, f32[4,35,256]{2,1,0:T(8,128)}, f32[1,1]{1,0:T(1,128)}) custom-call(f32[4,35,256]{2,1,0:T(8,128)} %copy.16.fields, f32[4,35,256]{2,1,0:T(8,128)} %copy.17.store, f32[9,256]{1,0:T(8,128)} %metric.1, f32[4,3,256]{2,1,0:T(4,128)} %copy.18.normals, f32[4,256]{1,0:T(4,128)} %scale.1, f32[1,256]{1,0:T(1,128)} %bitcast.4, ...), custom_call_target="tpu_custom_call" | custom-call | tf_op jit(solution)/shard_map/section/pallas_call | solution.py:521
  52.5 0.0 copy-start
  52.5 1.7 %copy.19 = f32[4,35,256]{2,0,1:T(4,128)} copy(f32[4,35,256]{2,1,0:T(8,128)} %get-tuple-element.9) | data formatting | bytes 286720
  54.2 0.0 copy-done
  54.2 0.7 %copy.20 = f32[4,35,256]{2,0,1:T(4,128)} copy(f32[4,35,256]{2,1,0:T(8,128)S(1)} %copy-done) | data formatting | bytes 286720
Async XLA Ops:
  1.9 1.6 %copy-start.1 = (f32[4,35,256]{2,0,1:T(4,128)S(1)}, f32[4,35,256]{2,0,1:T(4,128)}, u32[]{:S(2)}) copy-start(f32[4,35,256]{2,0,1:T(4,128)} %param.14) | copy-start | bytes 430084
  52.5 1.7 %copy-start = (f32[4,35,256]{2,1,0:T(8,128)S(1)}, f32[4,35,256]{2,1,0:T(8,128)}, u32[]{:S(2)}) copy-start(f32[4,35,256]{2,1,0:T(8,128)} %get-tuple-element.10) | copy-start | bytes 430084

commit v2 on v1

v2 whole, which is shorter than its diff:
```python
import functools

import jax
import jax.numpy as jnp
import numpy as np
from jax import lax
from jax.experimental import pallas as pl
from jax.experimental.pallas import tpu as pltpu
from jax.sharding import PartitionSpec as P

MESH = pl.DeviceIdType.MESH
F32 = jnp.float32
BF16 = jnp.bfloat16

RUNGE_CARRY = -567301805773.0 / 1357537059087.0
RUNGE_ADVANCE = 5161836677717.0 / 13612068292357.0
TIME_STEP = 0.02

NODES = 35
ELEMS = 256
FACES = 4 * ELEMS
NEAR = 4
NEAR_ROWS = 8 * 16


def pick_table():
    volume = [(a, b, c, 4 - a - b - c) for a in range(5) for b in range(5 - a) for c in range(5 - a - b)]
    triples = [(a, b, 4 - a - b) for a in range(5) for b in range(5 - a)]
    orders = [(0, 1, 2), (1, 2, 0), (2, 0, 1), (0, 2, 1), (2, 1, 0), (1, 0, 2)]
    inverse = [0, 2, 1, 3, 4, 5]
    table = np.zeros((4, 6, 16, 2, 48), np.float32)
    for facet in range(4):
        others = [corner for corner in range(4) if corner != facet]
        for option in range(6):
            order = orders[inverse[option]]
            for node in range(15):
                triple = triples[node]
                turned = tuple(triple[q] for q in order)
                corners = [0, 0, 0, 0]
                for place in range(3):
                    corners[others[place]] = turned[place]
                table[facet, option, node, :, volume.index(tuple(corners))] = 1.0
    return table.reshape(4, 96, 96)


def split(value):
    high = value.astype(BF16)
    low = (value - high.astype(F32)).astype(BF16)
    return high, low


def kernel(
    ng,
    ns,
    half,
    fields_hbm,
    store_hbm,
    metric_hbm,
    normals_hbm,
    scale_hbm,
    damping_hbm,
    mask_hbm,
    level_hbm,
    source_hbm,
    orient_hbm,
    deriv_hbm,
    lift_hbm,
    picks_hbm,
    fields_out,
    store_out,
    energy_out,
    fields,
    store,
    metric,
    normals,
    scale,
    damping,
    mask,
    level,
    source,
    orient,
    deriv,
    lift,
    picks,
    fields_new,
    store_new,
    stacked,
    inner,
    turned,
    place,
    local,
    base,
    lifts,
    near_box,
    far_box,
    grp_box,
    near_in,
    far_in,
    grp_in,
    stage,
    row_own,
    row_sub,
    sum_own,
    row_grp,
    load_sem,
    out_sem,
    near_sems,
    far_sems,
    grp_send,
    grp_recv,
    sub_sems,
    top_sems,
):
    g = lax.axis_index("grp")
    s = lax.axis_index("sub")
    far_at = NEAR_ROWS
    grp_at = NEAR_ROWS + 4 * (ns - 9)
    rows = grp_at + 32

    def load(at, src, dst):
        return pltpu.make_async_copy(src, dst, load_sem.at[at])

    load_source = load(0, source_hbm, source)
    load_orient = load(1, orient_hbm, orient)
    load_fields = [load(2 + c, fields_hbm.at[:, c, :], fields.at[c]) for c in range(4)]
    load_picks = load(6, picks_hbm, picks)
    load_store = [load(7 + c, store_hbm.at[:, c, :], store.at[c]) for c in range(4)]
    load_rest = [
        load(11, metric_hbm, metric),
        load(12, normals_hbm, normals),
        load(13, scale_hbm, scale),
        load(14, damping_hbm, damping),
        load(15, mask_hbm, mask),
        load(16, level_hbm, level),
        load(17, deriv_hbm, deriv),
        load(18, lift_hbm, lift),
    ]
    for copy in [load_source, load_orient, *load_fields, load_picks, *load_rest, *load_store]:
        copy.start()

    def peer(k):
        return lax.rem(s + k, ns)

    near_in[...] = jnp.zeros_like(near_in)
    far_in[...] = jnp.zeros_like(far_in)
    grp_in[...] = jnp.zeros_like(grp_in)

    order = sorted(range(1, ns), key=lambda k: -min(k, ns - k))

    barrier = pltpu.get_barrier_semaphore()
    for k in order:
        pl.semaphore_signal(barrier, inc=1, device_id=(g, peer(k)), device_id_type=MESH)
    for k in range(1, ng):
        pl.semaphore_signal(barrier, inc=1, device_id=(lax.rem(g + k, ng), s), device_id_type=MESH)

    load_source.wait()
    codes = jnp.concatenate([source[f : f + 1, :] for f in range(4)], axis=1)
    slot = codes - FACES
    block = slot >> 5
    rank = slot & 31
    delta = block - s
    delta = jnp.where(delta < 0, delta + ns, delta)
    in_sub = block < ns
    after = in_sub & (delta <= NEAR)
    before = in_sub & (delta >= ns - NEAR)
    apart = in_sub & (delta > NEAR) & (delta < ns - NEAR)
    box = jnp.where(after, (delta - 1) * 16, jnp.where(before, (delta - ns + 8) * 16, grp_at + (block - ns) * 16))
    row = jnp.where(apart, far_at + (delta - NEAR - 1) * 4 + (rank & 3), box + (rank & 15))
    row = row + half * jnp.where(apart, (rank >> 2) & 1, rank >> 4)
    row = jnp.where(codes >= FACES, row, -1)

    def build_place(i, carry):
        at = lax.broadcasted_iota(jnp.int32, (32, FACES), 0) + i * 32
        place[pl.ds(i * 32, 32), :] = jnp.where(at == row, 1.0, 0.0).astype(BF16)
        return carry

    lax.fori_loop(0, 2 * half // 32, build_place, 0)

    stacked[...] = jnp.zeros_like(stacked)
    load_orient.wait()
    load_picks.wait()
    for c in range(4):
        load_fields[c].wait()
        high, low = split(fields[c])
        stacked[c, 0:NODES, :] = high
        stacked[c, 48 : 48 + NODES, :] = low
    for f in range(4):
        option_of = orient[f : f + 1, :]
        at = slice(f * ELEMS, (f + 1) * ELEMS)
        for c in range(4):
            found = jnp.dot(picks[f], stacked[c], preferred_element_type=F32)
            inner[c * 16 : (c + 1) * 16, at] = found[0:16]
            chosen = found[0:16]
            for option in range(1, 6):
                chosen = jnp.where(option_of == option, found[option * 16 : (option + 1) * 16], chosen)
            high, low = split(chosen)
            turned[c * 16 : (c + 1) * 16, at] = high
            turned[64 + c * 16 : 64 + (c + 1) * 16, at] = low

    packed = lax.dot_general(place[...], turned[...], (((1,), (1,)), ((), ())), preferred_element_type=F32)
    left, right = packed[:half], packed[half:]
    left = left + pltpu.roll(left, 64, 1)
    right = right + pltpu.roll(right, 64, 1)
    lane = lax.broadcasted_iota(jnp.int32, (half, 128), 1)
    out = jnp.where(lane < 64, left, right)
    near_box[...] = out[:far_at].reshape(8, 16, 128)
    for b in range(ns - 9):
        far_box[b] = out[far_at + 4 * b : far_at + 4 * b + 4]
    grp_box[...] = out[grp_at:rows].reshape(2, 16, 128)

    pl.semaphore_wait(barrier, ns - 1 + ng - 1)

    def near_at(k):
        return k - 1 if k <= NEAR else k - ns + 8

    def sub_copy(k):
        if NEAR < k < ns - NEAR:
            src, dst, sems = far_box.at[k - NEAR - 1], far_in.at[ns - k - NEAR - 1], far_sems
        else:
            src, dst, sems = near_box.at[near_at(k)], near_in.at[near_at(ns - k)], near_sems
        return pltpu.make_async_remote_copy(
            src_ref=src,
            dst_ref=dst,
            send_sem=sems.at[0],
            recv_sem=sems.at[1],
            device_id=(g, peer(k)),
            device_id_type=MESH,
        )

    def grp_copy(up):
        return pltpu.make_async_remote_copy(
            src_ref=grp_box.at[up],
            dst_ref=grp_in.at[1 - up],
            send_sem=grp_send.at[up],
            recv_sem=grp_recv.at[1 - up],
            device_id=(g + 2 * up - 1, s),
            device_id_type=MESH,
        )

    for k in order:
        sub_copy(k).start()

    @pl.when(g < ng - 1)
    def _():
        grp_copy(1).start()

    @pl.when(g > 0)
    def _():
        grp_copy(0).start()

    for copy in [*load_rest, *load_store]:
        copy.wait()
    growth = jnp.exp2(level[...].astype(F32))
    absorb = damping[...] * mask[...].astype(F32)

    def build_local(i, carry):
        at = lax.broadcasted_iota(jnp.int32, (32, FACES), 0) + i * 32
        local[pl.ds(i * 32, 32), :] = jnp.where(at == codes, 1.0, 0.0).astype(BF16)
        return carry

    lax.fori_loop(0, FACES // 32, build_local, 0)
    outer_own = jnp.dot(turned[...], local[...], preferred_element_type=F32)

    lifts[...] = jnp.zeros_like(lifts)
    for f in range(4):
        lifts[0:NODES, f * 16 : f * 16 + 15] = lift[:, f * 15 : (f + 1) * 15]
    lift_high, lift_low = split(lifts[...])
    lift_cat = jnp.concatenate([lift_high, lift_high, lift_low], axis=1)

    slopes = [
        [jnp.dot(deriv[d], fields[c], precision=lax.Precision.HIGHEST, preferred_element_type=F32) for c in range(4)]
        for d in range(3)
    ]

    def physical(x, c):
        total = metric[3 * x : 3 * x + 1, :] * slopes[0][c]
        for y in range(1, 3):
            total = total + metric[3 * x + y : 3 * x + y + 1, :] * slopes[y][c]
        return growth * total

    volume = [-(physical(0, 1) + physical(1, 2) + physical(2, 3))]
    volume += [-physical(x, 0) for x in range(3)]
    for c in range(4):
        base[c] = RUNGE_CARRY * store[c] + TIME_STEP * (volume[c] - absorb * fields[c])

    def arrival(ref, sems):
        return pltpu.make_async_copy(ref, ref, sems.at[1])

    arrival(near_in, near_sems).wait()
    arrival(far_in, far_sems).wait()

    @pl.when(g > 0)
    def _():
        pltpu.make_async_copy(grp_in.at[0], grp_in.at[0], grp_recv.at[0]).wait()

    @pl.when(g < ng - 1)
    def _():
        pltpu.make_async_copy(grp_in.at[1], grp_in.at[1], grp_recv.at[1]).wait()

    stage[0:far_at, :] = near_in[...].reshape(far_at, 128)
    for b in range(ns - 9):
        stage[far_at + 4 * b : far_at + 4 * b + 4, :] = far_in[b]
    stage[grp_at:rows, :] = grp_in[...].reshape(32, 128)
    if stage.shape[0] > rows:
        stage[rows:, :] = jnp.zeros((stage.shape[0] - rows, 128), F32)
    came = stage[...].T
    came_high, came_low = split(came)
    left = jnp.concatenate([came_high[0:64], came_low[0:64]], axis=0)[:, :half]
    right = jnp.concatenate([came_high[64:128], came_low[64:128]], axis=0)[:, :half]
    outer_all = (
        outer_own
        + jnp.dot(left, place[0:half, :], preferred_element_type=F32)
        + jnp.dot(right, place[half : 2 * half, :], preferred_element_type=F32)
    )
    outer = outer_all[0:64] + outer_all[64:128]

    flux = [[None] * 4 for _ in range(4)]
    for f in range(4):
        at = slice(f * ELEMS, (f + 1) * ELEMS)
        wall = source[f : f + 1, :] < 0
        norm = [normals[x, f : f + 1, :] for x in range(3)]
        press_in = inner[0:16, at]
        veloc_in = [inner[(1 + x) * 16 : (2 + x) * 16, at] for x in range(3)]
        along = norm[0] * veloc_in[0] + norm[1] * veloc_in[1] + norm[2] * veloc_in[2]
        press_jump = jnp.where(wall, 0.0, press_in - outer[0:16, at])
        normal_jump = jnp.zeros_like(along)
        for x in range(3):
            met = jnp.where(wall, veloc_in[x] - 2.0 * norm[x] * along, outer[(1 + x) * 16 : (2 + x) * 16, at])
            normal_jump = normal_jump + norm[x] * (veloc_in[x] - met)
        weight = 0.5 * scale[f : f + 1, :] * growth
        flux[0][f] = weight * (normal_jump - press_jump)
        for x in range(3):
            flux[1 + x][f] = -norm[x] * flux[0][f]

    energy = jnp.zeros((1, ELEMS), F32)
    for c in range(4):
        high, low = split(jnp.concatenate(flux[c], axis=0))
        lifted = jnp.dot(lift_cat, jnp.concatenate([high, low, high], axis=0), preferred_element_type=F32)
        store_next = base[c] + TIME_STEP * lifted[0:NODES]
        fields_next = fields[c] + RUNGE_ADVANCE * store_next
        store_new[c] = store_next
        fields_new[c] = fields_next
        energy = energy + jnp.sum(fields_next * fields_next, axis=0, keepdims=True)
    energy = absorb * energy
    row_own[...] = energy[:, 0:128] + energy[:, 128:256]

    def sub_row(k):
        return pltpu.make_async_remote_copy(
            src_ref=row_own,
            dst_ref=row_sub.at[s],
            send_sem=sub_sems.at[0],
            recv_sem=sub_sems.at[1],
            device_id=(g, peer(k)),
            device_id_type=MESH,
        )

    for k in order:
        sub_row(k).start()
    row_sub[s] = row_own[...]

    outs = [pltpu.make_async_copy(fields_new.at[c], fields_out.at[:, c, :], out_sem.at[c]) for c in range(4)]
    outs += [pltpu.make_async_copy(store_new.at[c], store_out.at[:, c, :], out_sem.at[4 + c]) for c in range(4)]
    for copy in outs:
        copy.start()

    many = row_sub.at[0 : ns - 1]
    arrival(many, sub_sems).wait()
    sum_own[...] = jnp.sum(row_sub[...], axis=0)

    def top_row(k):
        return pltpu.make_async_remote_copy(
            src_ref=sum_own,
            dst_ref=row_grp.at[g],
            send_sem=top_sems.at[0],
            recv_sem=top_sems.at[1],
            device_id=(lax.rem(g + k, ng), s),
            device_id_type=MESH,
        )

    for k in sorted(range(1, ng), key=lambda k: -min(k, ng - k)):
        top_row(k).start()
    row_grp[g] = sum_own[...]

    def left_here(ref, sem):
        pltpu.make_async_copy(ref, ref, sem).wait()

    left_here(near_box, near_sems.at[0])
    left_here(far_box, far_sems.at[0])
    left_here(many, sub_sems.at[0])

    @pl.when(g < ng - 1)
    def _():
        grp_copy(1).wait_send()

    @pl.when(g > 0)
    def _():
        grp_copy(0).wait_send()

    for copy in outs:
        copy.wait()

    few = row_grp.at[0 : ng - 1]
    arrival(few, top_sems).wait()
    total = jnp.sum(jnp.sum(row_grp[...], axis=0))
    energy_out[0, 0] = total * (1.0 / (ELEMS * NODES * ng * ns))
    left_here(few, top_sems.at[0])


def solution(mesh):
    ng, ns = mesh.shape["grp"], mesh.shape["sub"]
    rows = NEAR_ROWS + 4 * (ns - 9) + 32
    half = -(-rows // 32) * 32
    both = ("grp", "sub")
    hbm = pl.BlockSpec(memory_space=pl.ANY)
    dma = pltpu.SemaphoreType.DMA
    volume = (4, NODES, ELEMS)
    state = jax.ShapeDtypeStruct((NODES, 4, ELEMS), F32)

    call = pl.pallas_call(
        functools.partial(kernel, ng, ns, half),
        out_shape=(state, state, jax.ShapeDtypeStruct((1, 1), F32)),
        in_specs=[hbm] * 13,
        out_specs=(hbm, hbm, pl.BlockSpec(memory_space=pltpu.SMEM)),
        scratch_shapes=[
            pltpu.VMEM(volume, F32),
            pltpu.VMEM(volume, F32),
            pltpu.VMEM((9, ELEMS), F32),
            pltpu.VMEM((3, 4, ELEMS), F32),
            pltpu.VMEM((4, ELEMS), F32),
            pltpu.VMEM((1, ELEMS), F32),
            pltpu.VMEM((1, ELEMS), jnp.int32),
            pltpu.VMEM((1, ELEMS), jnp.int32),
            pltpu.VMEM((4, ELEMS), jnp.int32),
            pltpu.VMEM((4, ELEMS), jnp.int32),
            pltpu.VMEM((3, NODES, NODES), F32),
            pltpu.VMEM((NODES, 60), F32),
            pltpu.VMEM((4, 96, 96), BF16),
            pltpu.VMEM(volume, F32),
            pltpu.VMEM(volume, F32),
            pltpu.VMEM((4, 96, ELEMS), BF16),
            pltpu.VMEM((64, FACES), F32),
            pltpu.VMEM((128, FACES), BF16),
            pltpu.VMEM((2 * half, FACES), BF16),
            pltpu.VMEM((FACES, FACES), BF16),
            pltpu.VMEM(volume, F32),
            pltpu.VMEM((48, 64), F32),
            pltpu.VMEM((8, 16, 128), F32),
            pltpu.VMEM((ns - 9, 4, 128), F32),
            pltpu.VMEM((2, 16, 128), F32),
            pltpu.VMEM((8, 16, 128), F32),
            pltpu.VMEM((ns - 9, 4, 128), F32),
            pltpu.VMEM((2, 16, 128), F32),
            pltpu.VMEM((-(-half // 128) * 128, 128), F32),
            pltpu.VMEM((1, 128), F32),
            pltpu.VMEM((ns, 1, 128), F32),
            pltpu.VMEM((1, 128), F32),
            pltpu.VMEM((ng, 1, 128), F32),
            dma((19,)),
            dma((8,)),
            dma((2,)),
            dma((2,)),
            dma((2,)),
            dma((2,)),
            dma((2,)),
            dma((2,)),
        ],
        compiler_params=pltpu.CompilerParams(collective_id=0, has_side_effects=True),
        name="section",
    )

    def local(
        fields,
        section_store,
        metric_terms,
        normals,
        face_scale,
        damping,
        absorb_mask,
        refine_level,
        face_source,
        orientation,
        derivative,
        lift_matrix,
    ):
        fields_next, store_next, energy = call(
            jnp.transpose(fields, (1, 0, 2)),
            jnp.transpose(section_store, (1, 0, 2)),
            metric_terms,
            jnp.transpose(normals, (1, 0, 2)),
            face_scale,
            damping.reshape(1, ELEMS),
            absorb_mask.reshape(1, ELEMS),
            refine_level.reshape(1, ELEMS),
            face_source,
            orientation,
            derivative,
            lift_matrix,
            jnp.asarray(pick_table(), BF16),
        )
        return (
            jnp.transpose(fields_next, (1, 0, 2)),
            jnp.transpose(store_next, (1, 0, 2)),
            energy.reshape(()),
        )

    in_specs = (
        P(None, None, both),
        P(None, None, both),
        P(None, both),
        P(None, None, both),
        P(None, both),
        P(both),
        P(both),
        P(both),
        P(None, both),
        P(None, both),
        P(),
        P(),
    )
    out_specs = (P(None, None, both), P(None, None, both), P())
    return jax.shard_map(local, mesh=mesh, in_specs=in_specs, out_specs=out_specs, check_vma=False)
```

time: 56.9 us -> 47.1 us (0.83)
  Pallas kernels: 48.2 us -> 42.2 us
  local copies, waits for them, and re-layouts: 6.04 us -> 2.28 us
    pallas_call x1, Pallas kernels: 48.2 us -> 42.2 us  [local(): call(jnp.transpose(fields, (1, 0, 2)), jnp.transpose(section_store, (1, 0...]
    unnamed x9 -> x4, local copies, waits for them, and re-layouts: 6.04 us -> 2.28 us
where the time goes in v2:
time: 47.1 us; the launch traced here: 47 us
  Pallas kernels  42.2 us (90%)
  between operations  2.47 us (5%)
  local copies, waits for them, and re-layouts  2.28 us (5%)
    pallas_call x1, Pallas kernels, local(): call(jnp.transpose(fields, (1, 0, 2)), jnp.transpose(section_store, (1, 0...  42.2 us
    unnamed x4, local copies, waits for them, and re-layouts  2.28 us

profile of v2, /device:TPU:1, one launch (start us, length us, event | category | flops | bytes accessed | tf_op | source)
XLA Modules:
  0.0 47.0 jit_solution(4661830113636890239)
XLA Ops:
  0.6 42.2 %section.1 = (f32[35,4,256]{2,1,0:T(4,128)}, f32[35,4,256]{2,1,0:T(4,128)}, f32[1,1]{1,0:T(1,128)}) custom-call(f32[35,4,256]{2,1,0:T(4,128)} %bitcast.11, f32[35,4,256]{2,1,0:T(4,128)} %bitcast.12, f32[9,256]{1,0:T(8,128)} %metric_hbm.1, f32[3,4,256]{2,1,0:T(4,128)} %bitcast.13, f32[4,256]{1,0:T(4,128)} %scale_hbm.1, f32[1,256]{1,0:T(1,128)} %bitcast.14, ...), custom_call_target="tpu_custom_call" | custom-call | tf_op jit(solution)/shard_map/section/pallas_call | solution.py:485
  42.8 0.0 copy-start
  42.9 1.6 %copy.19 = f32[4,35,256]{2,0,1:T(4,128)} copy(f32[4,35,256]{2,0,1:T(4,128)} %bitcast.10) | data formatting | bytes 286720
  44.5 0.0 copy-done
  44.5 0.7 %copy.20 = f32[4,35,256]{2,0,1:T(4,128)} copy(f32[4,35,256]{2,0,1:T(4,128)S(1)} %bitcast.9) | data formatting | bytes 286720
Async XLA Ops:
  42.8 1.6 %copy-start = (f32[35,4,256]{2,1,0:T(4,128)S(1)}, f32[35,4,256]{2,1,0:T(4,128)}, u32[]{:S(2)}) copy-start(f32[35,4,256]{2,1,0:T(4,128)} %get-tuple-element.7) | copy-start | bytes 430084

commit v3 on v2

--- a/solution.py
+++ b/solution.py
@@ -66,9 +66,9 @@
     deriv_hbm,
     lift_hbm,
     picks_hbm,
-    fields_out,
-    store_out,
-    energy_out,
+    fields_new,
+    store_new,
+    energy_row,
     fields,
     store,
     metric,
@@ -82,8 +82,6 @@
     deriv,
     lift,
     picks,
-    fields_new,
-    store_new,
     stacked,
     inner,
     turned,
@@ -97,13 +95,13 @@
     near_in,
     far_in,
     grp_in,
-    stage,
+    near_stage,
+    far_stage,
     row_own,
     row_sub,
     sum_own,
     row_grp,
     load_sem,
-    out_sem,
     near_sems,
     far_sems,
     grp_send,
@@ -113,9 +111,9 @@
 ):
     g = lax.axis_index("grp")
     s = lax.axis_index("sub")
-    far_at = NEAR_ROWS
-    grp_at = NEAR_ROWS + 4 * (ns - 9)
-    rows = grp_at + 32
+    grp_at = NEAR_ROWS
+    far_at = NEAR_ROWS + 32
+    rows = far_at + 4 * (ns - 9)
 
     def load(at, src, dst):
         return pltpu.make_async_copy(src, dst, load_sem.at[at])
@@ -139,7 +137,12 @@
         copy.start()
 
     def peer(k):
-        return lax.rem(s + k, ns)
+        other = s + k
+        return jnp.where(other >= ns, other - ns, other)
+
+    def peer_grp(k):
+        other = g + k
+        return jnp.where(other >= ng, other - ng, other)
 
     near_in[...] = jnp.zeros_like(near_in)
     far_in[...] = jnp.zeros_like(far_in)
@@ -151,7 +154,7 @@
     for k in order:
         pl.semaphore_signal(barrier, inc=1, device_id=(g, peer(k)), device_id_type=MESH)
     for k in range(1, ng):
-        pl.semaphore_signal(barrier, inc=1, device_id=(lax.rem(g + k, ng), s), device_id_type=MESH)
+        pl.semaphore_signal(barrier, inc=1, device_id=(peer_grp(k), s), device_id_type=MESH)
 
     load_source.wait()
     codes = jnp.concatenate([source[f : f + 1, :] for f in range(4)], axis=1)
@@ -203,10 +206,10 @@
     right = right + pltpu.roll(right, 64, 1)
     lane = lax.broadcasted_iota(jnp.int32, (half, 128), 1)
     out = jnp.where(lane < 64, left, right)
-    near_box[...] = out[:far_at].reshape(8, 16, 128)
+    near_box[...] = out[:grp_at].reshape(8, 16, 128)
     for b in range(ns - 9):
         far_box[b] = out[far_at + 4 * b : far_at + 4 * b + 4]
-    grp_box[...] = out[grp_at:rows].reshape(2, 16, 128)
+    grp_box[...] = out[grp_at:far_at].reshape(2, 16, 128)
 
     pl.semaphore_wait(barrier, ns - 1 + ng - 1)
 
@@ -286,8 +289,18 @@
     def arrival(ref, sems):
         return pltpu.make_async_copy(ref, ref, sems.at[1])
 
+    def picked(stage, at):
+        came = stage[...].T
+        high, low = split(came)
+        deep = stage.shape[0]
+        left = jnp.concatenate([high[0:64], low[0:64]], axis=0)
+        right = jnp.concatenate([high[64:128], low[64:128]], axis=0)
+        return jnp.dot(left, place[at : at + deep, :], preferred_element_type=F32) + jnp.dot(
+            right, place[half + at : half + at + deep, :], preferred_element_type=F32
+        )
+
+    far_stage[...] = jnp.zeros_like(far_stage)
     arrival(near_in, near_sems).wait()
-    arrival(far_in, far_sems).wait()
 
     @pl.when(g > 0)
     def _():
@@ -297,21 +310,14 @@
     def _():
         pltpu.make_async_copy(grp_in.at[1], grp_in.at[1], grp_recv.at[1]).wait()
 
-    stage[0:far_at, :] = near_in[...].reshape(far_at, 128)
+    near_stage[0:grp_at, :] = near_in[...].reshape(grp_at, 128)
+    near_stage[grp_at:far_at, :] = grp_in[...].reshape(32, 128)
+    outer_near = outer_own + picked(near_stage, 0)
+
+    arrival(far_in, far_sems).wait()
     for b in range(ns - 9):
-        stage[far_at + 4 * b : far_at + 4 * b + 4, :] = far_in[b]
-    stage[grp_at:rows, :] = grp_in[...].reshape(32, 128)
-    if stage.shape[0] > rows:
-        stage[rows:, :] = jnp.zeros((stage.shape[0] - rows, 128), F32)
-    came = stage[...].T
-    came_high, came_low = split(came)
-    left = jnp.concatenate([came_high[0:64], came_low[0:64]], axis=0)[:, :half]
-    right = jnp.concatenate([came_high[64:128], came_low[64:128]], axis=0)[:, :half]
-    outer_all = (
-        outer_own
-        + jnp.dot(left, place[0:half, :], preferred_element_type=F32)
-        + jnp.dot(right, place[half : 2 * half, :], preferred_element_type=F32)
-    )
+        far_stage[4 * b : 4 * b + 4, :] = far_in[b]
+    outer_all = outer_near + picked(far_stage, far_at)
     outer = outer_all[0:64] + outer_all[64:128]
 
     flux = [[None] * 4 for _ in range(4)]
@@ -358,11 +364,6 @@
         sub_row(k).start()
     row_sub[s] = row_own[...]
 
-    outs = [pltpu.make_async_copy(fields_new.at[c], fields_out.at[:, c, :], out_sem.at[c]) for c in range(4)]
-    outs += [pltpu.make_async_copy(store_new.at[c], store_out.at[:, c, :], out_sem.at[4 + c]) for c in range(4)]
-    for copy in outs:
-        copy.start()
-
     many = row_sub.at[0 : ns - 1]
     arrival(many, sub_sems).wait()
     sum_own[...] = jnp.sum(row_sub[...], axis=0)
@@ -373,7 +374,7 @@
             dst_ref=row_grp.at[g],
             send_sem=top_sems.at[0],
             recv_sem=top_sems.at[1],
-            device_id=(lax.rem(g + k, ng), s),
+            device_id=(peer_grp(k), s),
             device_id_type=MESH,
         )
 
@@ -396,31 +397,42 @@
     def _():
         grp_copy(0).wait_send()
 
+    few = row_grp.at[0 : ng - 1]
+    arrival(few, top_sems).wait()
+    energy_row[...] = jnp.sum(row_grp[...], axis=0)
+    left_here(few, top_sems.at[0])
+
+
+def finish(count, fields_new, store_new, energy_row, fields_out, store_out, energy_out, out_sem):
+    outs = [pltpu.make_async_copy(fields_new.at[c], fields_out.at[:, c, :], out_sem.at[c]) for c in range(4)]
+    outs += [pltpu.make_async_copy(store_new.at[c], store_out.at[:, c, :], out_sem.at[4 + c]) for c in range(4)]
+    for copy in outs:
+        copy.start()
+    energy_out[0, 0] = jnp.sum(energy_row[...]) * (1.0 / count)
     for copy in outs:
         copy.wait()
-
-    few = row_grp.at[0 : ng - 1]
-    arrival(few, top_sems).wait()
-    total = jnp.sum(jnp.sum(row_grp[...], axis=0))
-    energy_out[0, 0] = total * (1.0 / (ELEMS * NODES * ng * ns))
-    left_here(few, top_sems.at[0])
 
 
 def solution(mesh):
     ng, ns = mesh.shape["grp"], mesh.shape["sub"]
     rows = NEAR_ROWS + 4 * (ns - 9) + 32
-    half = -(-rows // 32) * 32
+    half = -(-rows // 16) * 16
     both = ("grp", "sub")
-    hbm = pl.BlockSpec(memory_space=pl.ANY)
+    hbm = pl.BlockSpec(memory_space=pltpu.HBM)
+    vmem = pl.BlockSpec(memory_space=pltpu.VMEM)
     dma = pltpu.SemaphoreType.DMA
     volume = (4, NODES, ELEMS)
     state = jax.ShapeDtypeStruct((NODES, 4, ELEMS), F32)
 
     call = pl.pallas_call(
         functools.partial(kernel, ng, ns, half),
-        out_shape=(state, state, jax.ShapeDtypeStruct((1, 1), F32)),
+        out_shape=(
+            jax.ShapeDtypeStruct(volume, F32),
+            jax.ShapeDtypeStruct(volume, F32),
+            jax.ShapeDtypeStruct((1, 128), F32),
+        ),
         in_specs=[hbm] * 13,
-        out_specs=(hbm, hbm, pl.BlockSpec(memory_space=pltpu.SMEM)),
+        out_specs=(vmem, vmem, vmem),
         scratch_shapes=[
             pltpu.VMEM(volume, F32),
             pltpu.VMEM(volume, F32),
@@ -435,8 +447,6 @@
             pltpu.VMEM((3, NODES, NODES), F32),
             pltpu.VMEM((NODES, 60), F32),
             pltpu.VMEM((4, 96, 96), BF16),
-            pltpu.VMEM(volume, F32),
-            pltpu.VMEM(volume, F32),
             pltpu.VMEM((4, 96, ELEMS), BF16),
             pltpu.VMEM((64, FACES), F32),
             pltpu.VMEM((128, FACES), BF16),
@@ -450,13 +460,13 @@
             pltpu.VMEM((8, 16, 128), F32),
             pltpu.VMEM((ns - 9, 4, 128), F32),
             pltpu.VMEM((2, 16, 128), F32),
-            pltpu.VMEM((-(-half // 128) * 128, 128), F32),
+            pltpu.VMEM((NEAR_ROWS + 32, 128), F32),
+            pltpu.VMEM((half - NEAR_ROWS - 32, 128), F32),
             pltpu.VMEM((1, 128), F32),
             pltpu.VMEM((ns, 1, 128), F32),
             pltpu.VMEM((1, 128), F32),
             pltpu.VMEM((ng, 1, 128), F32),
             dma((19,)),
-            dma((8,)),
             dma((2,)),
             dma((2,)),
             dma((2,)),
@@ -464,9 +474,21 @@
             dma((2,)),
             dma((2,)),
         ],
-        compiler_params=pltpu.CompilerParams(collective_id=0, has_side_effects=True),
+        compiler_params=pltpu.CompilerParams(collective_id=0, has_side_effects=True, vmem_limit_bytes=24 << 20),
         name="section",
     )
+    write = pl.pallas_call(
+        functools.partial(finish, ELEMS * NODES * ng * ns),
+        out_shape=(state, state, jax.ShapeDtypeStruct((1, 1), F32)),
+        in_specs=[vmem] * 3,
+        out_specs=(hbm, hbm, pl.BlockSpec(memory_space=pltpu.SMEM)),
+        scratch_shapes=[dma((8,))],
+        compiler_params=pltpu.CompilerParams(vmem_limit_bytes=8 << 20),
+        name="finish",
+    )
+
+    def keep(x):
+        return pltpu.with_memory_space_constraint(x, pltpu.HBM)
 
     def local(
         fields,
@@ -482,7 +504,7 @@
         derivative,
         lift_matrix,
     ):
-        fields_next, store_next, energy = call(
+        fields_new, store_new, energy_row = call(*map(keep,(
             jnp.transpose(fields, (1, 0, 2)),
             jnp.transpose(section_store, (1, 0, 2)),
             metric_terms,
@@ -496,7 +518,8 @@
             derivative,
             lift_matrix,
             jnp.asarray(pick_table(), BF16),
-        )
+        )))
+        fields_next, store_next, energy = write(fields_new, store_new, energy_row)
         return (
             jnp.transpose(fields_next, (1, 0, 2)),
             jnp.transpose(store_next, (1, 0, 2)),

time: 47.1 us -> 43.2 us (0.917)
  local copies, waits for them, and re-layouts: 2.28 us -> 0 us
  between operations: 2.47 us -> 0.64 us
    unnamed x4 -> x0, local copies, waits for them, and re-layouts: 2.28 us -> none
    pallas_call x1 -> x2, Pallas kernels: 42.2 us -> 42.4 us  [the longest x1 41.1 us: local(): call(*map(keep, (jnp.transpose(fields, (1, 0, 2)), jnp.transpose(section_...]
where the time goes in v3:
time: 43.2 us; the launch traced here: 43 us
  Pallas kernels  42.4 us (98%)
  between operations  0.64 us (1%)
    pallas_call x1, Pallas kernels, local(): call(*map(keep, (jnp.transpose(fields, (1, 0, 2)), jnp.transpose(section_...  41.1 us
    pallas_call x1, Pallas kernels, local(): fields_next, store_next, energy = write(fields_new, store_new, energy_row)  1.31 us

profile of v3, /device:TPU:1, one launch (start us, length us, event | category | flops | bytes accessed | tf_op | source)
XLA Modules:
  0.0 43.0 jit_solution(7363632444870731564)
XLA Ops:
  0.6 41.1 %section.1 = (f32[4,35,256]{2,1,0:T(8,128)S(1)}, f32[4,35,256]{2,1,0:T(8,128)S(1)}, f32[1,128]{1,0:T(1,128)S(1)}) custom-call(f32[35,4,256]{2,1,0:T(4,128)} %bitcast.9, f32[35,4,256]{2,1,0:T(4,128)} %bitcast.10, f32[9,256]{1,0:T(8,128)} %metric_hbm.1, f32[3,4,256]{2,1,0:T(4,128)} %bitcast.11, f32[4,256]{1,0:T(4,128)} %scale_hbm.1, f32[1,256]{1,0:T(1,128)} %bitcast.12, ...), custom_call_target="tpu_custom_call" | custom-call | tf_op jit(solution)/shard_map/section/pallas_call | solution.py:507
  41.7 1.3 %finish.1 = (f32[35,4,256]{2,1,0:T(4,128)}, f32[35,4,256]{2,1,0:T(4,128)}, f32[1,1]{1,0:T(1,128)}) custom-call(f32[4,35,256]{2,1,0:T(8,128)S(1)} %get-tuple-element.9.fields_new, f32[4,35,256]{2,1,0:T(8,128)S(1)} %get-tuple-element.10.store_new, f32[1,128]{1,0:T(1,128)S(1)} %get-tuple-element.11.energy_row), custom_call_target="tpu_custom_call" | custom-call | tf_op jit(solution)/shard_map/finish/pallas_call | solution.py:522

commit v4 on v3

--- a/solution.py
+++ b/solution.py
@@ -19,8 +19,9 @@
 NODES = 35
 ELEMS = 256
 FACES = 4 * ELEMS
-NEAR = 4
-NEAR_ROWS = 8 * 16
+RING = 4
+NEAR_BOXES = 11
+NEAR_ROWS = NEAR_BOXES * 16
 
 
 def pick_table():
@@ -95,6 +96,7 @@
     near_in,
     far_in,
     grp_in,
+    relay_in,
     near_stage,
     far_stage,
     row_own,
@@ -108,12 +110,17 @@
     grp_recv,
     sub_sems,
     top_sems,
+    relay_sems,
+    pass_sem,
 ):
     g = lax.axis_index("grp")
     s = lax.axis_index("sub")
     grp_at = NEAR_ROWS
     far_at = NEAR_ROWS + 32
-    rows = far_at + 4 * (ns - 9)
+    far_count = ns - 3 * RING
+    nz = ns // RING
+    z = s // RING
+    x = s % RING
 
     def load(at, src, dst):
         return pltpu.make_async_copy(src, dst, load_sem.at[at])
@@ -133,42 +140,53 @@
         load(17, deriv_hbm, deriv),
         load(18, lift_hbm, lift),
     ]
-    for copy in [load_source, load_orient, *load_fields, load_picks, *load_rest, *load_store]:
+    for copy in [load_source, load_orient, *load_fields, load_picks]:
         copy.start()
 
-    def peer(k):
-        other = s + k
-        return jnp.where(other >= ns, other - ns, other)
+    def wrapped(value, count):
+        return jnp.where(value >= count, value - count, value)
+
+    z_at = [wrapped(z + dz, nz) for dz in range(nz)]
+    x_at = [(x + dx) % RING for dx in range(RING)]
+
+    def peer(dz, dx):
+        return z_at[dz % nz] * RING + x_at[dx % RING]
 
     def peer_grp(k):
-        other = g + k
-        return jnp.where(other >= ng, other - ng, other)
-
+        return wrapped(g + k, ng)
+
+    def hops(dz, dx):
+        return min(dz % nz, -dz % nz) + min(dx % RING, -dx % RING)
+
+    def farthest(pairs):
+        return sorted(pairs, key=lambda pair: -hops(*pair))
+
+    everyone = farthest([(dz, dx) for dz in range(nz) for dx in range(RING) if (dz, dx) != (0, 0)])
+    close = [(dz, dx) for dz, dx in everyone if min(dz, nz - dz) <= 3]
+
+    barrier = pltpu.get_barrier_semaphore()
+    greeted = [(hops(dz, dx), (g, peer(dz, dx))) for dz, dx in close]
+    greeted += [(min(k, ng - k) // 2, (peer_grp(k), s)) for k in range(1, ng)]
     near_in[...] = jnp.zeros_like(near_in)
-    far_in[...] = jnp.zeros_like(far_in)
     grp_in[...] = jnp.zeros_like(grp_in)
-
-    order = sorted(range(1, ns), key=lambda k: -min(k, ns - k))
-
-    barrier = pltpu.get_barrier_semaphore()
-    for k in order:
-        pl.semaphore_signal(barrier, inc=1, device_id=(g, peer(k)), device_id_type=MESH)
-    for k in range(1, ng):
-        pl.semaphore_signal(barrier, inc=1, device_id=(peer_grp(k), s), device_id_type=MESH)
+    for _, device in sorted(greeted, key=lambda entry: -entry[0]):
+        pl.semaphore_signal(barrier, inc=1, device_id=device, device_id_type=MESH)
+    for copy in [*load_rest, *load_store]:
+        copy.start()
 
     load_source.wait()
     codes = jnp.concatenate([source[f : f + 1, :] for f in range(4)], axis=1)
     slot = codes - FACES
     block = slot >> 5
     rank = slot & 31
-    delta = block - s
-    delta = jnp.where(delta < 0, delta + ns, delta)
     in_sub = block < ns
-    after = in_sub & (delta <= NEAR)
-    before = in_sub & (delta >= ns - NEAR)
-    apart = in_sub & (delta > NEAR) & (delta < ns - NEAR)
-    box = jnp.where(after, (delta - 1) * 16, jnp.where(before, (delta - ns + 8) * 16, grp_at + (block - ns) * 16))
-    row = jnp.where(apart, far_at + (delta - NEAR - 1) * 4 + (rank & 3), box + (rank & 15))
+    dz = (block >> 2) - z
+    dz = jnp.where(dz < 0, dz + nz, dz)
+    dx = ((block & 3) - x) & 3
+    apart = in_sub & (dz > 1) & (dz < nz - 1)
+    box = jnp.where(dz == 0, dx - 1, jnp.where(dz == 1, 3 + dx, 7 + dx))
+    box = jnp.where(in_sub, box * 16, grp_at + (block - ns) * 16)
+    row = jnp.where(apart, far_at + ((dz - 2) * RING + dx) * 4 + (rank & 3), box + (rank & 15))
     row = row + half * jnp.where(apart, (rank >> 2) & 1, rank >> 4)
     row = jnp.where(codes >= FACES, row, -1)
 
@@ -206,27 +224,56 @@
     right = right + pltpu.roll(right, 64, 1)
     lane = lax.broadcasted_iota(jnp.int32, (half, 128), 1)
     out = jnp.where(lane < 64, left, right)
-    near_box[...] = out[:grp_at].reshape(8, 16, 128)
-    for b in range(ns - 9):
+    near_box[...] = out[:grp_at].reshape(NEAR_BOXES, 16, 128)
+    for b in range(far_count):
         far_box[b] = out[far_at + 4 * b : far_at + 4 * b + 4]
     grp_box[...] = out[grp_at:far_at].reshape(2, 16, 128)
 
-    pl.semaphore_wait(barrier, ns - 1 + ng - 1)
-
-    def near_at(k):
-        return k - 1 if k <= NEAR else k - ns + 8
-
-    def sub_copy(k):
-        if NEAR < k < ns - NEAR:
-            src, dst, sems = far_box.at[k - NEAR - 1], far_in.at[ns - k - NEAR - 1], far_sems
+    pl.semaphore_wait(barrier, len(greeted))
+
+    def near_at(dz, dx):
+        return {0: dx % RING - 1, 1: 3 + dx % RING, nz - 1: 7 + dx % RING}[dz % nz]
+
+    def far_slot(dz, dx):
+        return (dz % nz - 2) * RING + dx % RING
+
+    def sub_copy(dz, dx):
+        if 1 < dz < nz - 1:
+            src, dst, sems = far_box.at[far_slot(dz, dx)], far_in.at[far_slot(-dz, -dx)], far_sems
         else:
-            src, dst, sems = near_box.at[near_at(k)], near_in.at[near_at(ns - k)], near_sems
+            src, dst, sems = near_box.at[near_at(dz, dx)], near_in.at[near_at(-dz, -dx)], near_sems
         return pltpu.make_async_remote_copy(
             src_ref=src,
             dst_ref=dst,
             send_sem=sems.at[0],
             recv_sem=sems.at[1],
-            device_id=(g, peer(k)),
+            device_id=(g, peer(dz, dx)),
+            device_id_type=MESH,
+        )
+
+    relays = [(3, (5, 6)), (nz - 3, (7,)), (2, (4,)), (nz - 2, (8,))]
+
+    def relay_part(ref, legs, base):
+        return ref.at[far_slot(legs[0], 0) - base : far_slot(legs[-1], 0) + RING - base]
+
+    def relay_copy(n):
+        step, legs = relays[n]
+        return pltpu.make_async_remote_copy(
+            src_ref=relay_part(far_box, legs, 0),
+            dst_ref=relay_part(relay_in, legs, far_slot(4, 0)),
+            send_sem=far_sems.at[0],
+            recv_sem=relay_sems.at[n],
+            device_id=(g, peer(step, 0)),
+            device_id_type=MESH,
+        )
+
+    def forward_copy(step, leg, dx):
+        return pltpu.make_async_remote_copy(
+            src_ref=relay_in.at[far_slot(leg, dx) - far_slot(4, 0)],
+            dst_ref=far_in.at[far_slot(-leg, -dx)],
+            send_sem=pass_sem.at[0],
+            recv_sem=far_sems.at[1],
+            device_id=(g, peer(leg - step, dx)),
             device_id_type=MESH,
         )
 
@@ -240,8 +287,10 @@
             device_id_type=MESH,
         )
 
-    for k in order:
-        sub_copy(k).start()
+    for n in range(len(relays)):
+        relay_copy(n).start()
+    for dz, dx in close:
+        sub_copy(dz, dx).start()
 
     @pl.when(g < ng - 1)
     def _():
@@ -288,6 +337,16 @@
 
     def arrival(ref, sems):
         return pltpu.make_async_copy(ref, ref, sems.at[1])
+
+    for n, (step, legs) in enumerate(relays):
+        pltpu.make_async_copy(
+            relay_part(relay_in, legs, far_slot(4, 0)),
+            relay_part(relay_in, legs, far_slot(4, 0)),
+            relay_sems.at[n],
+        ).wait()
+        for dx in (2, 1, 3, 0):
+            for leg in reversed(legs):
+                forward_copy(step, leg, dx).start()
 
     def picked(stage, at):
         came = stage[...].T
@@ -299,7 +358,6 @@
             right, place[half + at : half + at + deep, :], preferred_element_type=F32
         )
 
-    far_stage[...] = jnp.zeros_like(far_stage)
     arrival(near_in, near_sems).wait()
 
     @pl.when(g > 0)
@@ -315,7 +373,7 @@
     outer_near = outer_own + picked(near_stage, 0)
 
     arrival(far_in, far_sems).wait()
-    for b in range(ns - 9):
+    for b in range(far_count):
         far_stage[4 * b : 4 * b + 4, :] = far_in[b]
     outer_all = outer_near + picked(far_stage, far_at)
     outer = outer_all[0:64] + outer_all[64:128]
@@ -350,18 +408,18 @@
     energy = absorb * energy
     row_own[...] = energy[:, 0:128] + energy[:, 128:256]
 
-    def sub_row(k):
+    def sub_row(dz, dx):
         return pltpu.make_async_remote_copy(
             src_ref=row_own,
             dst_ref=row_sub.at[s],
             send_sem=sub_sems.at[0],
             recv_sem=sub_sems.at[1],
-            device_id=(g, peer(k)),
+            device_id=(g, peer(dz, dx)),
             device_id_type=MESH,
         )
 
-    for k in order:
-        sub_row(k).start()
+    for dz, dx in everyone:
+        sub_row(dz, dx).start()
     row_sub[s] = row_own[...]
 
     many = row_sub.at[0 : ns - 1]
@@ -387,6 +445,7 @@
 
     left_here(near_box, near_sems.at[0])
     left_here(far_box, far_sems.at[0])
+    left_here(relay_in, pass_sem.at[0])
     left_here(many, sub_sems.at[0])
 
     @pl.when(g < ng - 1)
@@ -415,8 +474,8 @@
 
 def solution(mesh):
     ng, ns = mesh.shape["grp"], mesh.shape["sub"]
-    rows = NEAR_ROWS + 4 * (ns - 9) + 32
-    half = -(-rows // 16) * 16
+    far_count = ns - 3 * RING
+    half = NEAR_ROWS + 32 + 4 * far_count
     both = ("grp", "sub")
     hbm = pl.BlockSpec(memory_space=pltpu.HBM)
     vmem = pl.BlockSpec(memory_space=pltpu.VMEM)
@@ -454,12 +513,13 @@
             pltpu.VMEM((FACES, FACES), BF16),
             pltpu.VMEM(volume, F32),
             pltpu.VMEM((48, 64), F32),
-            pltpu.VMEM((8, 16, 128), F32),
-            pltpu.VMEM((ns - 9, 4, 128), F32),
+            pltpu.VMEM((NEAR_BOXES, 16, 128), F32),
+            pltpu.VMEM((far_count, 4, 128), F32),
             pltpu.VMEM((2, 16, 128), F32),
-            pltpu.VMEM((8, 16, 128), F32),
-            pltpu.VMEM((ns - 9, 4, 128), F32),
+            pltpu.VMEM((NEAR_BOXES, 16, 128), F32),
+            pltpu.VMEM((far_count, 4, 128), F32),
             pltpu.VMEM((2, 16, 128), F32),
+            pltpu.VMEM((5 * RING, 4, 128), F32),
             pltpu.VMEM((NEAR_ROWS + 32, 128), F32),
             pltpu.VMEM((half - NEAR_ROWS - 32, 128), F32),
             pltpu.VMEM((1, 128), F32),
@@ -473,6 +533,8 @@
             dma((2,)),
             dma((2,)),
             dma((2,)),
+            dma((4,)),
+            dma((1,)),
         ],
         compiler_params=pltpu.CompilerParams(collective_id=0, has_side_effects=True, vmem_limit_bytes=24 << 20),
         name="section",

time: 43.2 us -> 44.4 us (1.028)
  Pallas kernels: 42.4 us -> 43.6 us
    pallas_call x1, Pallas kernels: 41.1 us -> 42.3 us  [local(): call(*map(keep, (jnp.transpose(fields, (1, 0, 2)), jnp.transpose(section_...]
where the time goes in v4:
time: 44.4 us; the launch traced here: 44.2 us
  Pallas kernels  43.6 us (98%)
  between operations  0.64 us (1%)
    pallas_call x1, Pallas kernels, local(): call(*map(keep, (jnp.transpose(fields, (1, 0, 2)), jnp.transpose(section_...  42.3 us
    pallas_call x1, Pallas kernels, local(): fields_next, store_next, energy = write(fields_new, store_new, energy_row)  1.31 us

profile of v4, /device:TPU:1, one launch (start us, length us, event | category | flops | bytes accessed | tf_op | source)
XLA Modules:
  0.0 44.2 jit_solution(3256380706503516666)
XLA Ops:
  0.6 42.3 %section.1 = (f32[4,35,256]{2,1,0:T(8,128)S(1)}, f32[4,35,256]{2,1,0:T(8,128)S(1)}, f32[1,128]{1,0:T(1,128)S(1)}) custom-call(f32[35,4,256]{2,1,0:T(4,128)} %bitcast.9, f32[35,4,256]{2,1,0:T(4,128)} %bitcast.10, f32[9,256]{1,0:T(8,128)} %metric_hbm.1, f32[3,4,256]{2,1,0:T(4,128)} %bitcast.11, f32[4,256]{1,0:T(4,128)} %scale_hbm.1, f32[1,256]{1,0:T(1,128)} %bitcast.12, ...), custom_call_target="tpu_custom_call" | custom-call | tf_op jit(solution)/shard_map/section/pallas_call | solution.py:569
  42.9 1.3 %finish.1 = (f32[35,4,256]{2,1,0:T(4,128)}, f32[35,4,256]{2,1,0:T(4,128)}, f32[1,1]{1,0:T(1,128)}) custom-call(f32[4,35,256]{2,1,0:T(8,128)S(1)} %get-tuple-element.9.fields_new, f32[4,35,256]{2,1,0:T(8,128)S(1)} %get-tuple-element.10.store_new, f32[1,128]{1,0:T(1,128)S(1)} %get-tuple-element.11.energy_row), custom_call_target="tpu_custom_call" | custom-call | tf_op jit(solution)/shard_map/finish/pallas_call | solution.py:584

commit v5 on v4

--- a/solution.py
+++ b/solution.py
@@ -69,7 +69,7 @@
     picks_hbm,
     fields_new,
     store_new,
-    energy_row,
+    energy_new,
     fields,
     store,
     metric,
@@ -111,7 +111,7 @@
     sub_sems,
     top_sems,
     relay_sems,
-    pass_sem,
+    pass_sems,
 ):
     g = lax.axis_index("grp")
     s = lax.axis_index("sub")
@@ -164,13 +164,27 @@
     everyone = farthest([(dz, dx) for dz in range(nz) for dx in range(RING) if (dz, dx) != (0, 0)])
     close = [(dz, dx) for dz, dx in everyone if min(dz, nz - dz) <= 3]
 
+    relays = [(2, 4, 0, nz - 5), (3, 5, 0, nz - 6), (3, 6, 0, nz - 7), (nz - 3, 7, 3, 4), (nz - 2, 8, 2, 3)]
+
+    def relayed(n, step):
+        at = z_at[step % nz]
+        return (at >= relays[n][2]) & (at <= relays[n][3])
+
     barrier = pltpu.get_barrier_semaphore()
     greeted = [(hops(dz, dx), (g, peer(dz, dx))) for dz, dx in close]
     greeted += [(min(k, ng - k) // 2, (peer_grp(k), s)) for k in range(1, ng)]
-    near_in[...] = jnp.zeros_like(near_in)
     grp_in[...] = jnp.zeros_like(grp_in)
     for _, device in sorted(greeted, key=lambda entry: -entry[0]):
         pl.semaphore_signal(barrier, inc=1, device_id=device, device_id_type=MESH)
+    expected = len(greeted)
+    for n, (_, leg, _, _) in enumerate(relays):
+
+        @pl.when(jnp.logical_not(relayed(n, -leg)))
+        def _(leg=leg):
+            for dx in (2, 1, 3, 0):
+                pl.semaphore_signal(barrier, inc=1, device_id=(g, peer(-leg, dx)), device_id_type=MESH)
+
+        expected = expected + jnp.where(relayed(n, 0), 0, RING)
     for copy in [*load_rest, *load_store]:
         copy.start()
 
@@ -218,8 +232,9 @@
             turned[c * 16 : (c + 1) * 16, at] = high
             turned[64 + c * 16 : 64 + (c + 1) * 16, at] = low
 
-    packed = lax.dot_general(place[...], turned[...], (((1,), (1,)), ((), ())), preferred_element_type=F32)
-    left, right = packed[:half], packed[half:]
+    across = (((1,), (1,)), ((), ()))
+    left = lax.dot_general(place[:half, :], turned[...], across, preferred_element_type=F32)
+    right = lax.dot_general(place[half:, :], turned[...], across, preferred_element_type=F32)
     left = left + pltpu.roll(left, 64, 1)
     right = right + pltpu.roll(right, 64, 1)
     lane = lax.broadcasted_iota(jnp.int32, (half, 128), 1)
@@ -229,7 +244,7 @@
         far_box[b] = out[far_at + 4 * b : far_at + 4 * b + 4]
     grp_box[...] = out[grp_at:far_at].reshape(2, 16, 128)
 
-    pl.semaphore_wait(barrier, len(greeted))
+    pl.semaphore_wait(barrier, expected)
 
     def near_at(dz, dx):
         return {0: dx % RING - 1, 1: 3 + dx % RING, nz - 1: 7 + dx % RING}[dz % nz]
@@ -251,27 +266,26 @@
             device_id_type=MESH,
         )
 
-    relays = [(3, (5, 6)), (nz - 3, (7,)), (2, (4,)), (nz - 2, (8,))]
-
-    def relay_part(ref, legs, base):
-        return ref.at[far_slot(legs[0], 0) - base : far_slot(legs[-1], 0) + RING - base]
+    def relay_part(ref, leg, base):
+        return ref.at[far_slot(leg, 0) - base : far_slot(leg, 0) + RING - base]
 
     def relay_copy(n):
-        step, legs = relays[n]
+        step, leg, _, _ = relays[n]
         return pltpu.make_async_remote_copy(
-            src_ref=relay_part(far_box, legs, 0),
-            dst_ref=relay_part(relay_in, legs, far_slot(4, 0)),
+            src_ref=relay_part(far_box, leg, 0),
+            dst_ref=relay_part(relay_in, leg, far_slot(4, 0)),
             send_sem=far_sems.at[0],
             recv_sem=relay_sems.at[n],
             device_id=(g, peer(step, 0)),
             device_id_type=MESH,
         )
 
-    def forward_copy(step, leg, dx):
+    def forward_copy(n, dx):
+        step, leg, _, _ = relays[n]
         return pltpu.make_async_remote_copy(
             src_ref=relay_in.at[far_slot(leg, dx) - far_slot(4, 0)],
             dst_ref=far_in.at[far_slot(-leg, -dx)],
-            send_sem=pass_sem.at[0],
+            send_sem=pass_sems.at[n],
             recv_sem=far_sems.at[1],
             device_id=(g, peer(leg - step, dx)),
             device_id_type=MESH,
@@ -287,8 +301,17 @@
             device_id_type=MESH,
         )
 
-    for n in range(len(relays)):
-        relay_copy(n).start()
+    for n, (_, leg, _, _) in enumerate(relays):
+
+        @pl.when(relayed(n, 0))
+        def _(n=n):
+            relay_copy(n).start()
+
+        @pl.when(jnp.logical_not(relayed(n, 0)))
+        def _(leg=leg):
+            for dx in (2, 1, 3, 0):
+                sub_copy(leg, dx).start()
+
     for dz, dx in close:
         sub_copy(dz, dx).start()
 
@@ -299,6 +322,15 @@
     @pl.when(g > 0)
     def _():
         grp_copy(0).start()
+
+    for n, (step, leg, _, _) in enumerate(relays):
+
+        @pl.when(relayed(n, -step))
+        def _(n=n, leg=leg):
+            part = relay_part(relay_in, leg, far_slot(4, 0))
+            pltpu.make_async_copy(part, part, relay_sems.at[n]).wait()
+            for dx in (2, 1, 3, 0):
+                forward_copy(n, dx).start()
 
     for copy in [*load_rest, *load_store]:
         copy.wait()
@@ -337,16 +369,6 @@
 
     def arrival(ref, sems):
         return pltpu.make_async_copy(ref, ref, sems.at[1])
-
-    for n, (step, legs) in enumerate(relays):
-        pltpu.make_async_copy(
-            relay_part(relay_in, legs, far_slot(4, 0)),
-            relay_part(relay_in, legs, far_slot(4, 0)),
-            relay_sems.at[n],
-        ).wait()
-        for dx in (2, 1, 3, 0):
-            for leg in reversed(legs):
-                forward_copy(step, leg, dx).start()
 
     def picked(stage, at):
         came = stage[...].T
@@ -445,7 +467,12 @@
 
     left_here(near_box, near_sems.at[0])
     left_here(far_box, far_sems.at[0])
-    left_here(relay_in, pass_sem.at[0])
+    for n, (step, leg, _, _) in enumerate(relays):
+
+        @pl.when(relayed(n, -step))
+        def _(n=n, leg=leg):
+            left_here(relay_part(relay_in, leg, far_slot(4, 0)), pass_sems.at[n])
+
     left_here(many, sub_sems.at[0])
 
     @pl.when(g < ng - 1)
@@ -458,16 +485,18 @@
 
     few = row_grp.at[0 : ng - 1]
     arrival(few, top_sems).wait()
-    energy_row[...] = jnp.sum(row_grp[...], axis=0)
+    total = jnp.sum(jnp.sum(row_grp[...], axis=0), axis=1, keepdims=True)
+    energy_new[...] = jnp.broadcast_to(total * (1.0 / (ELEMS * NODES * ng * ns)), (1, 128))
     left_here(few, top_sems.at[0])
 
 
-def finish(count, fields_new, store_new, energy_row, fields_out, store_out, energy_out, out_sem):
+def finish(fields_new, store_new, energy_new, fields_out, store_out, energy_out, single, out_sem):
+    single[...] = energy_new[:, 0:1]
     outs = [pltpu.make_async_copy(fields_new.at[c], fields_out.at[:, c, :], out_sem.at[c]) for c in range(4)]
     outs += [pltpu.make_async_copy(store_new.at[c], store_out.at[:, c, :], out_sem.at[4 + c]) for c in range(4)]
+    outs += [pltpu.make_async_copy(single, energy_out, out_sem.at[8])]
     for copy in outs:
         copy.start()
-    energy_out[0, 0] = jnp.sum(energy_row[...]) * (1.0 / count)
     for copy in outs:
         copy.wait()
 
@@ -533,18 +562,18 @@
             dma((2,)),
             dma((2,)),
             dma((2,)),
-            dma((4,)),
-            dma((1,)),
+            dma((5,)),
+            dma((5,)),
         ],
         compiler_params=pltpu.CompilerParams(collective_id=0, has_side_effects=True, vmem_limit_bytes=24 << 20),
         name="section",
     )
     write = pl.pallas_call(
-        functools.partial(finish, ELEMS * NODES * ng * ns),
+        finish,
         out_shape=(state, state, jax.ShapeDtypeStruct((1, 1), F32)),
         in_specs=[vmem] * 3,
-        out_specs=(hbm, hbm, pl.BlockSpec(memory_space=pltpu.SMEM)),
-        scratch_shapes=[dma((8,))],
+        out_specs=(hbm, hbm, hbm),
+        scratch_shapes=[pltpu.VMEM((1, 1), F32), dma((9,))],
         compiler_params=pltpu.CompilerParams(vmem_limit_bytes=8 << 20),
         name="finish",
     )
@@ -566,7 +595,7 @@
         derivative,
         lift_matrix,
     ):
-        fields_new, store_new, energy_row = call(*map(keep,(
+        fields_new, store_new, energy_new = call(*map(keep,(
             jnp.transpose(fields, (1, 0, 2)),
             jnp.transpose(section_store, (1, 0, 2)),
             metric_terms,
@@ -581,7 +610,7 @@
             lift_matrix,
             jnp.asarray(pick_table(), BF16),
         )))
-        fields_next, store_next, energy = write(fields_new, store_new, energy_row)
+        fields_next, store_next, energy = write(fields_new, store_new, energy_new)
         return (
             jnp.transpose(fields_next, (1, 0, 2)),
             jnp.transpose(store_next, (1, 0, 2)),

time: 44.4 us -> 45.6 us (1.027)
  Pallas kernels: 43.6 us -> 44.8 us
    pallas_call x1, Pallas kernels: 42.3 us -> 44 us  [local(): call(*map(keep, (jnp.transpose(fields, (1, 0, 2)), jnp.transpose(section_...]
    pallas_call x1, Pallas kernels: 1.31 us -> 0.8 us  [local(): fields_next, store_next, energy = write(fields_new, store_new, energy_new)]
where the time goes in v5:
time: 45.6 us; the launch traced here: 45.4 us
  Pallas kernels  44.8 us (98%)
  between operations  0.64 us (1%)
    pallas_call x1, Pallas kernels, local(): call(*map(keep, (jnp.transpose(fields, (1, 0, 2)), jnp.transpose(section_...  44 us

profile of v5, /device:TPU:1, one launch (start us, length us, event | category | flops | bytes accessed | tf_op | source)
XLA Modules:
  0.0 45.4 jit_solution(55337647098183646)
XLA Ops:
  0.6 44.0 %section.1 = (f32[4,35,256]{2,1,0:T(8,128)S(1)}, f32[4,35,256]{2,1,0:T(8,128)S(1)}, f32[1,128]{1,0:T(1,128)S(1)}) custom-call(f32[35,4,256]{2,1,0:T(4,128)} %bitcast.9, f32[35,4,256]{2,1,0:T(4,128)} %bitcast.10, f32[9,256]{1,0:T(8,128)} %metric_hbm.1, f32[3,4,256]{2,1,0:T(4,128)} %bitcast.11, f32[4,256]{1,0:T(4,128)} %scale_hbm.1, f32[1,256]{1,0:T(1,128)} %bitcast.12, ...), custom_call_target="tpu_custom_call" | custom-call | tf_op jit(solution)/shard_map/section/pallas_call | solution.py:598
  44.6 0.8 %finish.1 = (f32[35,4,256]{2,1,0:T(4,128)}, f32[35,4,256]{2,1,0:T(4,128)}, f32[1,1]{1,0:T(1,128)}) custom-call(f32[4,35,256]{2,1,0:T(8,128)S(1)} %get-tuple-element.9.fields_new, f32[4,35,256]{2,1,0:T(8,128)S(1)} %get-tuple-element.10.store_new, f32[1,128]{1,0:T(1,128)S(1)} %get-tuple-element.11.energy_new), custom_call_target="tpu_custom_call" | custom-call | tf_op jit(solution)/shard_map/finish/pallas_call | solution.py:613

commit v6 on v3

--- a/solution.py
+++ b/solution.py
@@ -68,7 +68,7 @@
     picks_hbm,
     fields_new,
     store_new,
-    energy_row,
+    energy_new,
     fields,
     store,
     metric,
@@ -89,6 +89,8 @@
     local,
     base,
     lifts,
+    deriv_pad,
+    deriv_cat,
     near_box,
     far_box,
     grp_box,
@@ -101,6 +103,8 @@
     row_sub,
     sum_own,
     row_grp,
+    total_own,
+    total_in,
     load_sem,
     near_sems,
     far_sems,
@@ -108,6 +112,8 @@
     grp_recv,
     sub_sems,
     top_sems,
+    up_sems,
+    down_sems,
 ):
     g = lax.axis_index("grp")
     s = lax.axis_index("sub")
@@ -133,9 +139,6 @@
         load(17, deriv_hbm, deriv),
         load(18, lift_hbm, lift),
     ]
-    for copy in [load_source, load_orient, *load_fields, load_picks, *load_rest, *load_store]:
-        copy.start()
-
     def peer(k):
         other = s + k
         return jnp.where(other >= ns, other - ns, other)
@@ -144,8 +147,6 @@
         other = g + k
         return jnp.where(other >= ng, other - ng, other)
 
-    near_in[...] = jnp.zeros_like(near_in)
-    far_in[...] = jnp.zeros_like(far_in)
     grp_in[...] = jnp.zeros_like(grp_in)
 
     order = sorted(range(1, ns), key=lambda k: -min(k, ns - k))
@@ -155,6 +156,9 @@
         pl.semaphore_signal(barrier, inc=1, device_id=(g, peer(k)), device_id_type=MESH)
     for k in range(1, ng):
         pl.semaphore_signal(barrier, inc=1, device_id=(peer_grp(k), s), device_id_type=MESH)
+
+    for copy in [load_source, load_orient, *load_fields, load_picks, *load_rest, *load_store]:
+        copy.start()
 
     load_source.wait()
     codes = jnp.concatenate([source[f : f + 1, :] for f in range(4)], axis=1)
@@ -200,8 +204,9 @@
             turned[c * 16 : (c + 1) * 16, at] = high
             turned[64 + c * 16 : 64 + (c + 1) * 16, at] = low
 
-    packed = lax.dot_general(place[...], turned[...], (((1,), (1,)), ((), ())), preferred_element_type=F32)
-    left, right = packed[:half], packed[half:]
+    across = (((1,), (1,)), ((), ()))
+    left = lax.dot_general(place[:half, :], turned[...], across, preferred_element_type=F32)
+    right = lax.dot_general(place[half:, :], turned[...], across, preferred_element_type=F32)
     left = left + pltpu.roll(left, 64, 1)
     right = right + pltpu.roll(right, 64, 1)
     lane = lax.broadcasted_iota(jnp.int32, (half, 128), 1)
@@ -270,10 +275,18 @@
     lift_high, lift_low = split(lifts[...])
     lift_cat = jnp.concatenate([lift_high, lift_high, lift_low], axis=1)
 
-    slopes = [
-        [jnp.dot(deriv[d], fields[c], precision=lax.Precision.HIGHEST, preferred_element_type=F32) for c in range(4)]
-        for d in range(3)
+    deriv_pad[...] = jnp.zeros_like(deriv_pad)
+    for d in range(3):
+        deriv_pad[48 * d : 48 * d + NODES, 0:NODES] = deriv[d]
+    deriv_high, deriv_low = split(deriv_pad[...])
+    deriv_cat[:, 0:48] = deriv_high
+    deriv_cat[:, 48:96] = deriv_high
+    found = [
+        jnp.dot(deriv_cat[...], stacked[c], preferred_element_type=F32)
+        + jnp.dot(deriv_low, stacked[c, 0:48, :], preferred_element_type=F32)
+        for c in range(4)
     ]
+    slopes = [[found[c][48 * d : 48 * d + NODES] for c in range(4)] for d in range(3)]
 
     def physical(x, c):
         total = metric[3 * x : 3 * x + 1, :] * slopes[0][c]
@@ -350,44 +363,67 @@
     energy = absorb * energy
     row_own[...] = energy[:, 0:128] + energy[:, 128:256]
 
-    def sub_row(k):
+    core = g % 2
+    level_y = g // 2
+    count_y = ng // 2
+    lead = 2 * level_y + 1
+
+    def sub_row(k, sems):
         return pltpu.make_async_remote_copy(
             src_ref=row_own,
-            dst_ref=row_sub.at[s],
-            send_sem=sub_sems.at[0],
+            dst_ref=row_sub.at[2 * s + core],
+            send_sem=sems.at[0],
             recv_sem=sub_sems.at[1],
-            device_id=(g, peer(k)),
+            device_id=(lead, peer(k)),
             device_id_type=MESH,
         )
 
     for k in order:
-        sub_row(k).start()
-    row_sub[s] = row_own[...]
-
-    many = row_sub.at[0 : ns - 1]
-    arrival(many, sub_sems).wait()
-    sum_own[...] = jnp.sum(row_sub[...], axis=0)
+        sub_row(k, sub_sems).start()
+
+    many = row_sub.at[0 : 2 * ns - 1]
+    rest = row_grp.at[0 : count_y - 1]
 
     def top_row(k):
+        other = level_y + k
         return pltpu.make_async_remote_copy(
             src_ref=sum_own,
-            dst_ref=row_grp.at[g],
+            dst_ref=row_grp.at[level_y],
             send_sem=top_sems.at[0],
             recv_sem=top_sems.at[1],
-            device_id=(peer_grp(k), s),
+            device_id=(2 * jnp.where(other >= count_y, other - count_y, other) + 1, s),
             device_id_type=MESH,
         )
 
-    for k in sorted(range(1, ng), key=lambda k: -min(k, ng - k)):
-        top_row(k).start()
-    row_grp[g] = sum_own[...]
+    def down_row():
+        return pltpu.make_async_remote_copy(
+            src_ref=total_own,
+            dst_ref=total_in,
+            send_sem=down_sems.at[0],
+            recv_sem=down_sems.at[1],
+            device_id=(2 * level_y, s),
+            device_id_type=MESH,
+        )
+
+    @pl.when(core == 0)
+    def _():
+        sub_row(0, up_sems).start()
+
+    @pl.when(core == 1)
+    def _():
+        row_sub[2 * s + 1] = row_own[...]
+        arrival(many, sub_sems).wait()
+        sum_own[...] = jnp.sum(row_sub[...], axis=0)
+        for k in sorted(range(1, count_y), key=lambda k: -min(k, count_y - k)):
+            top_row(k).start()
+        row_grp[level_y] = sum_own[...]
 
     def left_here(ref, sem):
         pltpu.make_async_copy(ref, ref, sem).wait()
 
     left_here(near_box, near_sems.at[0])
     left_here(far_box, far_sems.at[0])
-    left_here(many, sub_sems.at[0])
+    left_here(row_sub.at[0 : ns - 1], sub_sems.at[0])
 
     @pl.when(g < ng - 1)
     def _():
@@ -397,18 +433,30 @@
     def _():
         grp_copy(0).wait_send()
 
-    few = row_grp.at[0 : ng - 1]
-    arrival(few, top_sems).wait()
-    energy_row[...] = jnp.sum(row_grp[...], axis=0)
-    left_here(few, top_sems.at[0])
-
-
-def finish(count, fields_new, store_new, energy_row, fields_out, store_out, energy_out, out_sem):
+    @pl.when(core == 1)
+    def _():
+        arrival(rest, top_sems).wait()
+        total = jnp.sum(jnp.sum(row_grp[...], axis=0), axis=1, keepdims=True)
+        total_own[...] = jnp.broadcast_to(total * (1.0 / (ELEMS * NODES * ng * ns)), (1, 128))
+        down_row().start()
+        energy_new[...] = total_own[...]
+        left_here(rest, top_sems.at[0])
+        down_row().wait_send()
+
+    @pl.when(core == 0)
+    def _():
+        sub_row(0, up_sems).wait_send()
+        down_row().wait_recv()
+        energy_new[...] = total_in[...]
+
+
+def finish(fields_new, store_new, energy_new, fields_out, store_out, energy_out, single, out_sem):
+    single[...] = energy_new[:, 0:1]
     outs = [pltpu.make_async_copy(fields_new.at[c], fields_out.at[:, c, :], out_sem.at[c]) for c in range(4)]
     outs += [pltpu.make_async_copy(store_new.at[c], store_out.at[:, c, :], out_sem.at[4 + c]) for c in range(4)]
+    outs += [pltpu.make_async_copy(single, energy_out, out_sem.at[8])]
     for copy in outs:
         copy.start()
-    energy_out[0, 0] = jnp.sum(energy_row[...]) * (1.0 / count)
     for copy in outs:
         copy.wait()
 
@@ -454,6 +502,8 @@
             pltpu.VMEM((FACES, FACES), BF16),
             pltpu.VMEM(volume, F32),
             pltpu.VMEM((48, 64), F32),
+            pltpu.VMEM((144, 48), F32),
+            pltpu.VMEM((144, 96), BF16),
             pltpu.VMEM((8, 16, 128), F32),
             pltpu.VMEM((ns - 9, 4, 128), F32),
             pltpu.VMEM((2, 16, 128), F32),
@@ -463,26 +513,30 @@
             pltpu.VMEM((NEAR_ROWS + 32, 128), F32),
             pltpu.VMEM((half - NEAR_ROWS - 32, 128), F32),
             pltpu.VMEM((1, 128), F32),
-            pltpu.VMEM((ns, 1, 128), F32),
+            pltpu.VMEM((2 * ns, 1, 128), F32),
             pltpu.VMEM((1, 128), F32),
-            pltpu.VMEM((ng, 1, 128), F32),
+            pltpu.VMEM((ng // 2, 1, 128), F32),
+            pltpu.VMEM((1, 128), F32),
+            pltpu.VMEM((1, 128), F32),
             dma((19,)),
             dma((2,)),
             dma((2,)),
             dma((2,)),
             dma((2,)),
             dma((2,)),
+            dma((2,)),
+            dma((1,)),
             dma((2,)),
         ],
         compiler_params=pltpu.CompilerParams(collective_id=0, has_side_effects=True, vmem_limit_bytes=24 << 20),
         name="section",
     )
     write = pl.pallas_call(
-        functools.partial(finish, ELEMS * NODES * ng * ns),
+        finish,
         out_shape=(state, state, jax.ShapeDtypeStruct((1, 1), F32)),
         in_specs=[vmem] * 3,
-        out_specs=(hbm, hbm, pl.BlockSpec(memory_space=pltpu.SMEM)),
-        scratch_shapes=[dma((8,))],
+        out_specs=(hbm, hbm, hbm),
+        scratch_shapes=[pltpu.VMEM((1, 1), F32), dma((9,))],
         compiler_params=pltpu.CompilerParams(vmem_limit_bytes=8 << 20),
         name="finish",
     )
@@ -504,7 +558,7 @@
         derivative,
         lift_matrix,
     ):
-        fields_new, store_new, energy_row = call(*map(keep,(
+        fields_new, store_new, energy_new = call(*map(keep,(
             jnp.transpose(fields, (1, 0, 2)),
             jnp.transpose(section_store, (1, 0, 2)),
             metric_terms,
@@ -519,7 +573,7 @@
             lift_matrix,
             jnp.asarray(pick_table(), BF16),
         )))
-        fields_next, store_next, energy = write(fields_new, store_new, energy_row)
+        fields_next, store_next, energy = write(fields_new, store_new, energy_new)
         return (
             jnp.transpose(fields_next, (1, 0, 2)),
             jnp.transpose(store_next, (1, 0, 2)),

time: 43.2 us -> 42.6 us (0.986)
  Pallas kernels: 42.4 us -> 41.8 us
    pallas_call x1, Pallas kernels: 1.31 us -> 0.8 us  [local(): fields_next, store_next, energy = write(fields_new, store_new, energy_new)]
where the time goes in v6:
time: 42.6 us; the launch traced here: 42.4 us
  Pallas kernels  41.8 us (98%)
  between operations  0.64 us (2%)
    pallas_call x1, Pallas kernels, local(): call(*map(keep, (jnp.transpose(fields, (1, 0, 2)), jnp.transpose(section_...  41 us

profile of v6, /device:TPU:1, one launch (start us, length us, event | category | flops | bytes accessed | tf_op | source)
XLA Modules:
  0.0 42.4 jit_solution(8681216382401225574)
XLA Ops:
  0.6 41.0 %section.1 = (f32[4,35,256]{2,1,0:T(8,128)S(1)}, f32[4,35,256]{2,1,0:T(8,128)S(1)}, f32[1,128]{1,0:T(1,128)S(1)}) custom-call(f32[35,4,256]{2,1,0:T(4,128)} %bitcast.9, f32[35,4,256]{2,1,0:T(4,128)} %bitcast.10, f32[9,256]{1,0:T(8,128)} %metric_hbm.1, f32[3,4,256]{2,1,0:T(4,128)} %bitcast.11, f32[4,256]{1,0:T(4,128)} %scale_hbm.1, f32[1,256]{1,0:T(1,128)} %bitcast.12, ...), custom_call_target="tpu_custom_call" | custom-call | tf_op jit(solution)/shard_map/section/pallas_call | solution.py:561
  41.6 0.8 %finish.1 = (f32[35,4,256]{2,1,0:T(4,128)}, f32[35,4,256]{2,1,0:T(4,128)}, f32[1,1]{1,0:T(1,128)}) custom-call(f32[4,35,256]{2,1,0:T(8,128)S(1)} %get-tuple-element.9.fields_new, f32[4,35,256]{2,1,0:T(8,128)S(1)} %get-tuple-element.10.store_new, f32[1,128]{1,0:T(1,128)S(1)} %get-tuple-element.11.energy_new), custom_call_target="tpu_custom_call" | custom-call | tf_op jit(solution)/shard_map/finish/pallas_call | solution.py:576

commit v7 on v6

--- a/solution.py
+++ b/solution.py
@@ -20,6 +20,7 @@
 ELEMS = 256
 FACES = 4 * ELEMS
 NEAR = 4
+FAR_Y = 2
 NEAR_ROWS = 8 * 16
 
 
@@ -105,6 +106,7 @@
     row_grp,
     total_own,
     total_in,
+    row_first,
     load_sem,
     near_sems,
     far_sems,
@@ -114,6 +116,8 @@
     top_sems,
     up_sems,
     down_sems,
+    first_send,
+    first_recv,
 ):
     g = lax.axis_index("grp")
     s = lax.axis_index("sub")
@@ -378,9 +382,6 @@
             device_id_type=MESH,
         )
 
-    for k in order:
-        sub_row(k, sub_sems).start()
-
     many = row_sub.at[0 : 2 * ns - 1]
     rest = row_grp.at[0 : count_y - 1]
 
@@ -405,6 +406,26 @@
             device_id_type=MESH,
         )
 
+    first = (g == 1) & (s == 0)
+    far_y = (level_y >= FAR_Y) & (level_y <= count_y - FAR_Y)
+
+    def first_row():
+        return pltpu.make_async_remote_copy(
+            src_ref=row_own,
+            dst_ref=row_first.at[level_y, 2 * s + core],
+            send_sem=first_send.at[0],
+            recv_sem=first_recv.at[level_y],
+            device_id=(1, 0),
+            device_id_type=MESH,
+        )
+
+    @pl.when(far_y)
+    def _():
+        first_row().start()
+
+    for k in order:
+        sub_row(k, sub_sems).start()
+
     @pl.when(core == 0)
     def _():
         sub_row(0, up_sems).start()
@@ -415,7 +436,11 @@
         arrival(many, sub_sems).wait()
         sum_own[...] = jnp.sum(row_sub[...], axis=0)
         for k in sorted(range(1, count_y), key=lambda k: -min(k, count_y - k)):
-            top_row(k).start()
+
+            @pl.when(jnp.logical_not((s == 0) & far_y & (level_y + k == count_y)))
+            def _(k=k):
+                top_row(k).start()
+
         row_grp[level_y] = sum_own[...]
 
     def left_here(ref, sem):
@@ -433,15 +458,36 @@
     def _():
         grp_copy(0).wait_send()
 
+    @pl.when(far_y)
+    def _():
+        first_row().wait_send()
+
+    @pl.when(first)
+    def _():
+        arrival(row_grp.at[0 : 2 * FAR_Y - 2], top_sems).wait()
+        for y in sorted(range(FAR_Y, count_y - FAR_Y + 1), key=lambda y: min(y, count_y - y)):
+            pltpu.make_async_copy(row_first.at[y], row_first.at[y], first_recv.at[y]).wait()
+            row_grp[y] = jnp.sum(row_first[y], axis=0)
+
+    @pl.when((core == 1) & jnp.logical_not(first))
+    def _():
+        arrival(rest, top_sems).wait()
+
     @pl.when(core == 1)
     def _():
-        arrival(rest, top_sems).wait()
         total = jnp.sum(jnp.sum(row_grp[...], axis=0), axis=1, keepdims=True)
         total_own[...] = jnp.broadcast_to(total * (1.0 / (ELEMS * NODES * ng * ns)), (1, 128))
         down_row().start()
         energy_new[...] = total_own[...]
-        left_here(rest, top_sems.at[0])
         down_row().wait_send()
+
+        @pl.when((s == 0) & far_y)
+        def _():
+            left_here(row_grp.at[0 : count_y - 2], top_sems.at[0])
+
+        @pl.when(jnp.logical_not((s == 0) & far_y))
+        def _():
+            left_here(rest, top_sems.at[0])
 
     @pl.when(core == 0)
     def _():
@@ -518,6 +564,7 @@
             pltpu.VMEM((ng // 2, 1, 128), F32),
             pltpu.VMEM((1, 128), F32),
             pltpu.VMEM((1, 128), F32),
+            pltpu.VMEM((ng // 2, 2 * ns, 1, 128), F32),
             dma((19,)),
             dma((2,)),
             dma((2,)),
@@ -527,6 +574,8 @@
             dma((2,)),
             dma((1,)),
             dma((2,)),
+            dma((1,)),
+            dma((ng // 2,)),
         ],
         compiler_params=pltpu.CompilerParams(collective_id=0, has_side_effects=True, vmem_limit_bytes=24 << 20),
         name="section",

time: 42.6 us -> 41.4 us (0.972)
  Pallas kernels: 41.8 us -> 40.6 us
    pallas_call x1, Pallas kernels: 41 us -> 39.8 us  [local(): call(*map(keep, (jnp.transpose(fields, (1, 0, 2)), jnp.transpose(section_...]
where the time goes in v7:
time: 41.4 us; the launch traced here: 41.2 us
  Pallas kernels  40.6 us (98%)
  between operations  0.64 us (2%)
    pallas_call x1, Pallas kernels, local(): call(*map(keep, (jnp.transpose(fields, (1, 0, 2)), jnp.transpose(section_...  39.8 us

profile of v7, /device:TPU:1, one launch (start us, length us, event | category | flops | bytes accessed | tf_op | source)
XLA Modules:
  0.0 41.2 jit_solution(4896221420596189146)
XLA Ops:
  0.6 39.8 %section.1 = (f32[4,35,256]{2,1,0:T(8,128)S(1)}, f32[4,35,256]{2,1,0:T(8,128)S(1)}, f32[1,128]{1,0:T(1,128)S(1)}) custom-call(f32[35,4,256]{2,1,0:T(4,128)} %bitcast.9, f32[35,4,256]{2,1,0:T(4,128)} %bitcast.10, f32[9,256]{1,0:T(8,128)} %metric_hbm.1, f32[3,4,256]{2,1,0:T(4,128)} %bitcast.11, f32[4,256]{1,0:T(4,128)} %scale_hbm.1, f32[1,256]{1,0:T(1,128)} %bitcast.12, ...), custom_call_target="tpu_custom_call" | custom-call | tf_op jit(solution)/shard_map/section/pallas_call | solution.py:610
  40.4 0.8 %finish.1 = (f32[35,4,256]{2,1,0:T(4,128)}, f32[35,4,256]{2,1,0:T(4,128)}, f32[1,1]{1,0:T(1,128)}) custom-call(f32[4,35,256]{2,1,0:T(8,128)S(1)} %get-tuple-element.9.fields_new, f32[4,35,256]{2,1,0:T(8,128)S(1)} %get-tuple-element.10.store_new, f32[1,128]{1,0:T(1,128)S(1)} %get-tuple-element.11.energy_new), custom_call_target="tpu_custom_call" | custom-call | tf_op jit(solution)/shard_map/finish/pallas_call | solution.py:625

commit v8 on v7

--- a/solution.py
+++ b/solution.py
@@ -303,6 +303,31 @@
     for c in range(4):
         base[c] = RUNGE_CARRY * store[c] + TIME_STEP * (volume[c] - absorb * fields[c])
 
+    known = []
+    norms = []
+    shares = []
+    for f in range(4):
+        at = slice(f * ELEMS, (f + 1) * ELEMS)
+        wall = source[f : f + 1, :] < 0
+        norm = [normals[x, f : f + 1, :] for x in range(3)]
+        press_in = inner[0:16, at]
+        veloc_in = [inner[(1 + x) * 16 : (2 + x) * 16, at] for x in range(3)]
+        along = norm[0] * veloc_in[0] + norm[1] * veloc_in[1] + norm[2] * veloc_in[2]
+        square = norm[0] * norm[0] + norm[1] * norm[1] + norm[2] * norm[2]
+        weight = 0.5 * scale[f : f + 1, :] * growth
+        known.append(weight * jnp.where(wall, 2.0 * square * along, along - press_in))
+        share = jnp.where(wall, 0.0, weight)
+        norms.append(norm)
+        shares.append([share] + [-share * norm[x] for x in range(3)])
+
+    def weighed(part, f):
+        at = slice(f * ELEMS, (f + 1) * ELEMS)
+        total = 0.0
+        for c in range(4):
+            outer = part[c * 16 : (c + 1) * 16, at] + part[64 + c * 16 : 64 + (c + 1) * 16, at]
+            total = total + shares[f][c] * outer
+        return total
+
     def arrival(ref, sems):
         return pltpu.make_async_copy(ref, ref, sems.at[1])
 
@@ -331,29 +356,17 @@
     near_stage[grp_at:far_at, :] = grp_in[...].reshape(32, 128)
     outer_near = outer_own + picked(near_stage, 0)
 
+    known = [known[f] + weighed(outer_near, f) for f in range(4)]
+
     arrival(far_in, far_sems).wait()
     for b in range(ns - 9):
         far_stage[4 * b : 4 * b + 4, :] = far_in[b]
-    outer_all = outer_near + picked(far_stage, far_at)
-    outer = outer_all[0:64] + outer_all[64:128]
-
+    arrived = picked(far_stage, far_at)
     flux = [[None] * 4 for _ in range(4)]
     for f in range(4):
-        at = slice(f * ELEMS, (f + 1) * ELEMS)
-        wall = source[f : f + 1, :] < 0
-        norm = [normals[x, f : f + 1, :] for x in range(3)]
-        press_in = inner[0:16, at]
-        veloc_in = [inner[(1 + x) * 16 : (2 + x) * 16, at] for x in range(3)]
-        along = norm[0] * veloc_in[0] + norm[1] * veloc_in[1] + norm[2] * veloc_in[2]
-        press_jump = jnp.where(wall, 0.0, press_in - outer[0:16, at])
-        normal_jump = jnp.zeros_like(along)
+        flux[0][f] = known[f] + weighed(arrived, f)
         for x in range(3):
-            met = jnp.where(wall, veloc_in[x] - 2.0 * norm[x] * along, outer[(1 + x) * 16 : (2 + x) * 16, at])
-            normal_jump = normal_jump + norm[x] * (veloc_in[x] - met)
-        weight = 0.5 * scale[f : f + 1, :] * growth
-        flux[0][f] = weight * (normal_jump - press_jump)
-        for x in range(3):
-            flux[1 + x][f] = -norm[x] * flux[0][f]
+            flux[1 + x][f] = -norms[f][x] * flux[0][f]
 
     energy = jnp.zeros((1, ELEMS), F32)
     for c in range(4):

time: 41.4 us -> 41.4 us (level)
  no operation moved by 1% of the time
where the time goes in v8:
time: 41.4 us; the launch traced here: 41.2 us
  Pallas kernels  40.6 us (98%)
  between operations  0.64 us (2%)
    pallas_call x1, Pallas kernels, local(): call(*map(keep, (jnp.transpose(fields, (1, 0, 2)), jnp.transpose(section_...  39.8 us

profile of v8, /device:TPU:1, one launch (start us, length us, event | category | flops | bytes accessed | tf_op | source)
XLA Modules:
  0.0 41.2 jit_solution(1818545066648978078)
XLA Ops:
  0.6 39.8 %section.1 = (f32[4,35,256]{2,1,0:T(8,128)S(1)}, f32[4,35,256]{2,1,0:T(8,128)S(1)}, f32[1,128]{1,0:T(1,128)S(1)}) custom-call(f32[35,4,256]{2,1,0:T(4,128)} %bitcast.9, f32[35,4,256]{2,1,0:T(4,128)} %bitcast.10, f32[9,256]{1,0:T(8,128)} %metric_hbm.1, f32[3,4,256]{2,1,0:T(4,128)} %bitcast.11, f32[4,256]{1,0:T(4,128)} %scale_hbm.1, f32[1,256]{1,0:T(1,128)} %bitcast.12, ...), custom_call_target="tpu_custom_call" | custom-call | tf_op jit(solution)/shard_map/section/pallas_call | solution.py:623
  40.4 0.8 %finish.1 = (f32[35,4,256]{2,1,0:T(4,128)}, f32[35,4,256]{2,1,0:T(4,128)}, f32[1,1]{1,0:T(1,128)}) custom-call(f32[4,35,256]{2,1,0:T(8,128)S(1)} %get-tuple-element.9.fields_new, f32[4,35,256]{2,1,0:T(8,128)S(1)} %get-tuple-element.10.store_new, f32[1,128]{1,0:T(1,128)S(1)} %get-tuple-element.11.energy_new), custom_call_target="tpu_custom_call" | custom-call | tf_op jit(solution)/shard_map/finish/pallas_call | solution.py:638

commit v9 on v8

--- a/solution.py
+++ b/solution.py
@@ -158,8 +158,22 @@
     barrier = pltpu.get_barrier_semaphore()
     for k in order:
         pl.semaphore_signal(barrier, inc=1, device_id=(g, peer(k)), device_id_type=MESH)
-    for k in range(1, ng):
-        pl.semaphore_signal(barrier, inc=1, device_id=(peer_grp(k), s), device_id_type=MESH)
+    core = g % 2
+
+    def greet_grp(ks):
+        for k in ks:
+            pl.semaphore_signal(barrier, inc=1, device_id=(peer_grp(k), s), device_id_type=MESH)
+
+    @pl.when((core == 1) | (s == 0))
+    def _():
+        greet_grp(sorted(range(2, ng, 2), key=lambda k: -min(k, ng - k)))
+
+    @pl.when(s == 0)
+    def _():
+        greet_grp(range(3, ng - 1, 2))
+
+    greet_grp((1, ng - 1))
+    expected = ns + 1 + jnp.where((core == 1) | (s == 0), ng // 2 - 1, 0) + jnp.where(s == 0, ng // 2 - 2, 0)
 
     for copy in [load_source, load_orient, *load_fields, load_picks, *load_rest, *load_store]:
         copy.start()
@@ -220,7 +234,7 @@
         far_box[b] = out[far_at + 4 * b : far_at + 4 * b + 4]
     grp_box[...] = out[grp_at:far_at].reshape(2, 16, 128)
 
-    pl.semaphore_wait(barrier, ns - 1 + ng - 1)
+    pl.semaphore_wait(barrier, expected)
 
     def near_at(k):
         return k - 1 if k <= NEAR else k - ns + 8
@@ -380,7 +394,6 @@
     energy = absorb * energy
     row_own[...] = energy[:, 0:128] + energy[:, 128:256]
 
-    core = g % 2
     level_y = g // 2
     count_y = ng // 2
     lead = 2 * level_y + 1

time: 41.4 us -> 41.4 us (level)
  no operation moved by 1% of the time
where the time goes in v9:
time: 41.4 us; the launch traced here: 41.2 us
  Pallas kernels  40.6 us (98%)
  between operations  0.64 us (2%)
    pallas_call x1, Pallas kernels, local(): call(*map(keep, (jnp.transpose(fields, (1, 0, 2)), jnp.transpose(section_...  39.8 us

profile of v9, /device:TPU:1, one launch (start us, length us, event | category | flops | bytes accessed | tf_op | source)
XLA Modules:
  0.0 41.2 jit_solution(11019948017474631766)
XLA Ops:
  0.6 39.8 %section.1 = (f32[4,35,256]{2,1,0:T(8,128)S(1)}, f32[4,35,256]{2,1,0:T(8,128)S(1)}, f32[1,128]{1,0:T(1,128)S(1)}) custom-call(f32[35,4,256]{2,1,0:T(4,128)} %bitcast.9, f32[35,4,256]{2,1,0:T(4,128)} %bitcast.10, f32[9,256]{1,0:T(8,128)} %metric_hbm.1, f32[3,4,256]{2,1,0:T(4,128)} %bitcast.11, f32[4,256]{1,0:T(4,128)} %scale_hbm.1, f32[1,256]{1,0:T(1,128)} %bitcast.12, ...), custom_call_target="tpu_custom_call" | custom-call | tf_op jit(solution)/shard_map/section/pallas_call | solution.py:636
  40.4 0.8 %finish.1 = (f32[35,4,256]{2,1,0:T(4,128)}, f32[35,4,256]{2,1,0:T(4,128)}, f32[1,1]{1,0:T(1,128)}) custom-call(f32[4,35,256]{2,1,0:T(8,128)S(1)} %get-tuple-element.9.fields_new, f32[4,35,256]{2,1,0:T(8,128)S(1)} %get-tuple-element.10.store_new, f32[1,128]{1,0:T(1,128)S(1)} %get-tuple-element.11.energy_new), custom_call_target="tpu_custom_call" | custom-call | tf_op jit(solution)/shard_map/finish/pallas_call | solution.py:651
